TPU v7x, 256 devices: a 2x2x32 block of a 4x8x32 slice. The times are simulated.
256 devices in a mesh: pop: 4 (over x, y), chain: 64 (over z, core).
Axes of the slice: x: 2, y: 2, z: 32, core: 2. Of those that a mesh axis runs over, the one named last changes fastest.
The devices are a block of a 4x8x32 slice.
Arguments:
- cost: float32 [65536, 4096], P(('pop', 'chain')), parts along dimension 0, may hold values from 0 to 20
- marginals: float32 [65536], P(('pop', 'chain')), parts along dimension 0, may hold values from 0.125 to 6
- final_marginal: float32 [16384], P('pop'), parts along dimension 0, may hold values from 0.125 to 6
Outputs:
- log_scaling: float32 [65536], P(('pop', 'chain')), parts along dimension 0
There are 4 independent parts, one for each index of `pop`. A program takes and returns all parts, laid end to end along the dimension named above; each array names one. Nothing has to cross between parts.
All inputs are finite; a program needn't handle non-finite values.
Results may differ from a plain program's by a relative error of at most 0.0001.
Values sent between devices are 32-bit elements; how exact they have to be, the bound alone decides.
A program may use at most 64 MiB of HBM per device.

v0:
```python
import jax
import jax.numpy as jnp
from jax import lax
from jax.sharding import PartitionSpec as P

SWEEPS = 2


entropic = 0.25


def swapped(value, axis, apart):
    return lax.ppermute(value, axis, [(i, i ^ 1 << apart) for i in range(lax.axis_size(axis))])


def from_behind(block, axis, distance):
    devices = range(lax.axis_size(axis))
    route = [(i - distance, i) for i in devices if i - distance in devices]
    return lax.ppermute(block, axis, route)


def butterfly_sum(vector, width):
    for bit_index in range(width.bit_length() - 1):
        vector = vector + swapped(vector, "chain", bit_index)
    return vector


def doubling_gather(first, second, member, width):
    for bit_index in range(width.bit_length() - 1):
        other_first, other_second = swapped((first, second), "chain", bit_index)
        upward = member >> bit_index & 1 == 1
        first = jnp.where(
            upward, jnp.concatenate([other_first, first]), jnp.concatenate([first, other_first])
        )
        second = jnp.where(
            upward, jnp.concatenate([other_second, second]), jnp.concatenate([second, other_second])
        )
    return (first, second)


def on_device(cost, marginals, final_marginal):
    row_count = cost.shape[0]
    states = cost.shape[1]
    width = states // row_count
    kernels = lax.axis_size("chain") // width
    index = lax.axis_index("chain")
    group = index // width
    member = index % width
    kernel = jnp.exp(-cost / entropic)
    scaling = jnp.ones((row_count,), jnp.float32)
    last_scaling = jnp.ones((states,), jnp.float32)
    for sweep_index in range(SWEEPS):
        current = scaling
        alpha_start = jnp.ones((states,), jnp.float32)
        forward_state = (jnp.ones((row_count,), jnp.float32), current, alpha_start)
        backward_state = (jnp.ones((row_count,), jnp.float32), last_scaling)
        for position in range(kernels):
            partial_sums = jnp.dot(
                forward_state[1],
                kernel,
                precision=lax.Precision.HIGHEST,
                preferred_element_type=jnp.float32,
            )
            whole = butterfly_sum(partial_sums, width)
            forward_whole_alpha = whole * (states / jnp.sum(whole))
            forward_outgoing = lax.dynamic_slice_in_dim(
                forward_whole_alpha, member * row_count, row_count
            )
            forward_alpha_block, carried, forward_alpha_last = forward_state
            if position == kernels - 1:
                forward_alpha_last = forward_whole_alpha
            if position < kernels - 1:
                forward_arrived = from_behind(forward_outgoing, "chain", width)
                taking = group == position + 1
                forward_alpha_block = jnp.where(taking, forward_arrived, forward_alpha_block)
                carried = jnp.where(taking, current * forward_arrived, carried)
            forward_state = (forward_alpha_block, carried, forward_alpha_last)
        for position in range(kernels):
            backward_raw = jnp.dot(
                kernel,
                backward_state[1],
                precision=lax.Precision.HIGHEST,
                preferred_element_type=jnp.float32,
            )
            backward_raw_full, backward_weighted_full = doubling_gather(
                backward_raw, current * backward_raw, member, width
            )
            backward_beta_block, carried_full = backward_state
            target_step = kernels - 1 - position
            factor = states / jnp.sum(backward_raw_full)
            backward_beta_block = jnp.where(
                group == target_step, backward_raw * factor, backward_beta_block
            )
            if target_step > 0:
                arrived = from_behind(backward_weighted_full * factor, "chain", -width)
                carried_full = jnp.where(group == target_step - 1, arrived, carried_full)
            backward_state = (backward_beta_block, carried_full)
        alpha_block, carried_unused, alpha_last = forward_state
        beta_block = backward_state[0]
        scaling = marginals / (alpha_block * beta_block)
        last_scaling = final_marginal / alpha_last
    return jnp.log(scaling)


def solution(mesh):
    placed = (P(("pop", "chain"), None), P(("pop", "chain")), P("pop"))
    return jax.shard_map(
        on_device, mesh=mesh, in_specs=placed, out_specs=P(("pop", "chain")), check_vma=False
    )
```

profile of v0, /device:TPU:44, one launch (start us, length us, event | category | flops | bytes accessed | tf_op | source)
XLA Modules:
  0.0 406.8 jit_solution(13602544734672436421)
XLA Ops:
  0.0 5.7 %fusion.14 = f32[1,256]{1,0:T(1,128)S(1)} fusion(f32[256,4096]{1,0:T(8,128)} %param.3), kind=kOutput, calls=%fused_computation.38 | convolution fusion | flops 14680064 | bytes 4195328 | tf_op jit(solution)/shard_map/dot_general | solution.py:79
  10.6 3.7 collective-permute-start.17
  14.3 4.6 %fusion.17 = f32[1,4096]{1,0:T(1,128)S(1)} fusion(f32[256,4096]{1,0:T(8,128)} %param.3), kind=kOutput, calls=%fused_computation.82 | convolution fusion | flops 14680064 | bytes 4210688 | tf_op jit(solution)/shard_map/dot_general | solution.py:58
  19.0 8.1 %collective-permute-start.18 = (f32[2048]{0:T(1024)S(1)}, f32[2048]{0:T(1024)S(1)}, u32[]{:S(2)}, u32[]{:S(2)}) collective-permute-start(f32[2048]{0:T(1024)S(1)} %maximum_select_fusion.11), channel_id=1, source_target_pairs={{0,8},{1,9},{2,10},{3,11},{4,12},{5,13},{6,14},{7,15},{8,0},{9,1},... | collective-permute-start | bytes 24584 | tf_op jit(solution)/shard_map/ppermute | solution.py:13
  34.0 17.3 %collective-permute-done.19 = f32[4096]{0:T(1024)S(1)} collective-permute-done((f32[4096]{0:T(1024)S(1)}, f32[4096]{0:T(1024)S(1)}, u32[]{:S(2)}, u32[]{:S(2)}) %collective-permute-start.19) | collective-permute-done | bytes 16416 | tf_op jit(solution)/shard_map/ppermute | solution.py:19
  51.3 6.5 %collective-permute-start.3 = (f32[4096]{0:T(1024)S(1)}, f32[4096]{0:T(1024)S(1)}, u32[]{:S(2)}, u32[]{:S(2)}) collective-permute-start(f32[4096]{0:T(1024)S(1)} %add.99), channel_id=1, source_target_pairs={{0,8},{1,9},{2,10},{3,11},{4,12},{5,13},{6,14},{7,15},{8,0},{9,1},... | collective-permute-start | bytes 49160 | tf_op jit(solution)/shard_map/ppermute | solution.py:13
  57.9 5.7 %fusion.31 = f32[1,256]{1,0:T(1,128)S(1)} fusion(f32[4096,1]{0,1:T(1,128)S(1)} %bitcast.61, f32[256,4096]{1,0:T(8,128)} %param.3), kind=kOutput, calls=%fused_computation.96 | convolution fusion | flops 14680064 | bytes 4211712 | tf_op jit(solution)/shard_map/dot_general | solution.py:79
  65.0 12.6 %collective-permute-start.4 = (f32[256]{0:T(256)S(1)}, f32[256]{0:T(256)S(1)}, u32[]{:S(2)}, u32[]{:S(2)}) collective-permute-start(f32[256]{0:T(256)S(1)} %dynamic-slice_multiply_fusion.5), channel_id=1, source_target_pairs={{0,16},{1,17},{2,18},{3,19},{4,20},{5,21},{6,22},{7,23},{8,24},{9,... | collective-permute-start | bytes 3080 | tf_op jit(solution)/shard_map/ppermute | solution.py:19
  78.9 4.6 %fusion.33 = f32[1,4096]{1,0:T(1,128)S(1)} fusion(f32[256,1]{0,1:T(1,128)S(1)} %bitcast.93, f32[256,4096]{1,0:T(8,128)} %param.3), kind=kOutput, calls=%fused_computation.98 | convolution fusion | flops 14680064 | bytes 4211712 | tf_op jit(solution)/shard_map/dot_general | solution.py:58
  85.7 2.6 collective-permute-done.22
  90.2 5.7 %collective-permute-done.23 = f32[2048]{0:T(1024)S(1)} collective-permute-done((f32[2048]{0:T(1024)S(1)}, f32[2048]{0:T(1024)S(1)}, u32[]{:S(2)}, u32[]{:S(2)}) %collective-permute-start.23) | collective-permute-done | bytes 8224 | tf_op jit(solution)/shard_map/ppermute | solution.py:13
  98.7 3.3 collective-permute-done.7
  103.8 8.4 %collective-permute-done.24 = f32[4096]{0:T(1024)S(1)} collective-permute-done((f32[4096]{0:T(1024)S(1)}, f32[4096]{0:T(1024)S(1)}, u32[]{:S(2)}, u32[]{:S(2)}) %collective-permute-start.24) | collective-permute-done | bytes 16416 | tf_op jit(solution)/shard_map/ppermute | solution.py:19
  113.6 13.2 %collective-permute-start.9 = (f32[256]{0:T(256)S(1)}, f32[256]{0:T(256)S(1)}, u32[]{:S(2)}, u32[]{:S(2)}) collective-permute-start(f32[256]{0:T(256)S(1)} %dynamic-slice_multiply_fusion.4), channel_id=1, source_target_pairs={{0,16},{1,17},{2,18},{3,19},{4,20},{5,21},{6,22},{7,23},{8,24},{9,... | collective-permute-start | bytes 3080 | tf_op jit(solution)/shard_map/ppermute | solution.py:19
  126.8 5.7 %fusion.30 = f32[1,256]{1,0:T(1,128)S(1)} fusion(f32[4096,1]{0,1:T(1,128)S(1)} %bitcast.42, f32[256,4096]{1,0:T(8,128)} %param.3), kind=kOutput, calls=%fused_computation.95 | convolution fusion | flops 14680064 | bytes 4211712 | tf_op jit(solution)/shard_map/dot_general | solution.py:79
  132.6 2.4 fusion.32
  139.3 2.6 collective-permute-start.27
  145.7 5.7 %collective-permute-done.28 = f32[2048]{0:T(1024)S(1)} collective-permute-done((f32[2048]{0:T(1024)S(1)}, f32[2048]{0:T(1024)S(1)}, u32[]{:S(2)}, u32[]{:S(2)}) %collective-permute-start.28) | collective-permute-done | bytes 8224 | tf_op jit(solution)/shard_map/ppermute | solution.py:13
  156.0 4.4 %collective-permute-done.13 = f32[4096]{0:T(1024)S(1)} collective-permute-done((f32[4096]{0:T(1024)S(1)}, f32[4096]{0:T(1024)S(1)}, u32[]{:S(2)}, u32[]{:S(2)}) %collective-permute-start.13) | collective-permute-done | bytes 16416 | tf_op jit(solution)/shard_map/ppermute | solution.py:13
  161.8 12.0 %collective-permute-start.14 = (f32[256]{0:T(256)S(1)}, f32[256]{0:T(256)S(1)}, u32[]{:S(2)}, u32[]{:S(2)}) collective-permute-start(f32[256]{0:T(256)S(1)} %dynamic-slice_multiply_fusion.3), channel_id=1, source_target_pairs={{0,16},{1,17},{2,18},{3,19},{4,20},{5,21},{6,22},{7,23},{8,24},{9,... | collective-permute-start | bytes 3080 | tf_op jit(solution)/shard_map/ppermute | solution.py:19
  174.9 4.7 %fusion.25 = f32[1,4096]{1,0:T(1,128)S(1)} fusion(f32[256,1]{0,1:T(1,128)S(1)} %bitcast.77, f32[256,4096]{1,0:T(8,128)} %param.3), kind=kOutput, calls=%fused_computation.90 | convolution fusion | flops 14680064 | bytes 4211712 | tf_op jit(solution)/shard_map/dot_general | solution.py:58
  179.6 3.5 fusion.29
  192.2 2.9 collective-permute-start.52
  195.1 3.4 collective-permute-start.33
  198.5 4.6 %collective-permute-done.33 = f32[2048]{0:T(1024)S(1)} collective-permute-done((f32[2048]{0:T(1024)S(1)}, f32[2048]{0:T(1024)S(1)}, u32[]{:S(2)}, u32[]{:S(2)}) %collective-permute-start.33) | collective-permute-done | bytes 8224 | tf_op jit(solution)/shard_map/ppermute | solution.py:13
  205.7 5.9 %fusion.24 = f32[1,256]{1,0:T(1,128)S(1)} fusion(f32[4096,1]{0,1:T(1,128)S(1)} %bitcast.41, f32[256,4096]{1,0:T(8,128)} %param.3), kind=kOutput, calls=%fused_computation.89 | convolution fusion | flops 14680064 | bytes 4211712 | tf_op jit(solution)/shard_map/dot_general | solution.py:79
  211.6 2.4 fusion.28
  221.1 2.6 collective-permute-done.36
  223.7 3.0 collective-permute-start.37
  228.3 3.1 collective-permute-done.37
  232.7 12.9 %collective-permute-start.38 = (f32[256]{0:T(256)S(1)}, f32[256]{0:T(256)S(1)}, u32[]{:S(2)}, u32[]{:S(2)}) collective-permute-start(f32[256]{0:T(256)S(1)} %dynamic-slice_multiply_fusion.2), channel_id=1, source_target_pairs={{0,16},{1,17},{2,18},{3,19},{4,20},{5,21},{6,22},{7,23},{8,24},{9,... | collective-permute-start | bytes 3080 | tf_op jit(solution)/shard_map/ppermute | solution.py:19
  247.0 4.6 %fusion.27 = f32[1,4096]{1,0:T(1,128)S(1)} fusion(f32[256,1]{0,1:T(1,128)S(1)} %bitcast.76, f32[256,4096]{1,0:T(8,128)} %param.3), kind=kOutput, calls=%fused_computation.92 | convolution fusion | flops 14680064 | bytes 4211712 | tf_op jit(solution)/shard_map/dot_general | solution.py:58
  251.8 3.5 collective-permute-start.60
  255.9 2.9 collective-permute-start.56
  265.6 3.5 collective-permute-start.42
  269.1 8.8 %collective-permute-done.61 = f32[4096]{0:T(1024)S(1)} collective-permute-done((f32[4096]{0:T(1024)S(1)}, f32[4096]{0:T(1024)S(1)}, u32[]{:S(2)}, u32[]{:S(2)}) %collective-permute-start.61) | collective-permute-done | bytes 16416 | tf_op jit(solution)/shard_map/ppermute | solution.py:19
  279.3 12.3 %collective-permute-start.43 = (f32[256]{0:T(256)S(1)}, f32[256]{0:T(256)S(1)}, u32[]{:S(2)}, u32[]{:S(2)}) collective-permute-start(f32[256]{0:T(256)S(1)} %dynamic-slice_multiply_fusion.1), channel_id=1, source_target_pairs={{0,16},{1,17},{2,18},{3,19},{4,20},{5,21},{6,22},{7,23},{8,24},{9,... | collective-permute-start | bytes 3080 | tf_op jit(solution)/shard_map/ppermute | solution.py:19
  291.6 5.7 %fusion.23 = f32[1,256]{1,0:T(1,128)S(1)} fusion(f32[4096,1]{0,1:T(1,128)S(1)} %bitcast.43, f32[256,4096]{1,0:T(8,128)} %param.3), kind=kOutput, calls=%fused_computation.88 | convolution fusion | flops 14680064 | bytes 4211712 | tf_op jit(solution)/shard_map/dot_general | solution.py:79
  307.0 2.7 collective-permute-start.69
  309.7 3.3 collective-permute-start.65
  318.6 13.2 %collective-permute-done.70 = f32[4096]{0:T(1024)S(1)} collective-permute-done((f32[4096]{0:T(1024)S(1)}, f32[4096]{0:T(1024)S(1)}, u32[]{:S(2)}, u32[]{:S(2)}) %collective-permute-start.70) | collective-permute-done | bytes 16416 | tf_op jit(solution)/shard_map/ppermute | solution.py:19
  331.8 5.7 %fusion.22 = f32[1,256]{1,0:T(1,128)S(1)} fusion(f32[4096,1]{0,1:T(1,128)S(1)} %bitcast.44, f32[256,4096]{1,0:T(8,128)} %param.3), kind=kOutput, calls=%fused_computation.87 | convolution fusion | flops 14680064 | bytes 4211712 | tf_op jit(solution)/shard_map/dot_general | solution.py:79
  346.8 3.8 collective-permute-start.78
  361.7 11.1 %collective-permute-done.79 = f32[4096]{0:T(1024)S(1)} collective-permute-done((f32[4096]{0:T(1024)S(1)}, f32[4096]{0:T(1024)S(1)}, u32[]{:S(2)}, u32[]{:S(2)}) %collective-permute-start.79) | collective-permute-done | bytes 16416 | tf_op jit(solution)/shard_map/ppermute | solution.py:19
  372.7 5.7 %fusion.21 = f32[1,256]{1,0:T(1,128)S(1)} fusion(f32[4096,1]{0,1:T(1,128)S(1)} %bitcast.60, f32[256,4096]{1,0:T(8,128)} %param.3), kind=kOutput, calls=%fused_computation.86 | convolution fusion | flops 14680064 | bytes 4211712 | tf_op jit(solution)/shard_map/dot_general | solution.py:79
  383.3 2.4 collective-permute-start.47
  387.1 4.2 %collective-permute-done.47 = f32[4096]{0:T(1024)S(1)} collective-permute-done((f32[4096]{0:T(1024)S(1)}, f32[4096]{0:T(1024)S(1)}, u32[]{:S(2)}, u32[]{:S(2)}) %collective-permute-start.47) | collective-permute-done | bytes 16416 | tf_op jit(solution)/shard_map/ppermute | solution.py:13
  394.9 9.5 %collective-permute-start.48 = (f32[256]{0:T(256)S(1)}, f32[256]{0:T(256)S(1)}, u32[]{:S(2)}, u32[]{:S(2)}) collective-permute-start(f32[256]{0:T(256)S(1)} %dynamic-slice_multiply_fusion), channel_id=1, source_target_pairs={{0,16},{1,17},{2,18},{3,19},{4,20},{5,21},{6,22},{7,23},{8,24},{9,... | collective-permute-start | bytes 3080 | tf_op jit(solution)/shard_map/ppermute | solution.py:19
  (243 shorter events, 108.5 us)
Async XLA Ops:
  10.6 8.4 %collective-permute-start.17 = (f32[1024]{0:T(1024)S(1)}, f32[1024]{0:T(1024)S(1)}, u32[]{:S(2)}, u32[]{:S(2)}) collective-permute-start(f32[1024]{0:T(1024)S(1)} %maximum_select_fusion.22), channel_id=1, source_target_pairs={{0,4},{1,5},{2,6},{3,7},{4,0},{5,1},{6,2},{7,3},{8,12},{9,13},{10,... | collective-permute-start | bytes 12296 | tf_op jit(solution)/shard_map/ppermute | solution.py:13
  18.9 11.2 %collective-permute-start = (f32[4096]{0:T(1024)S(1)}, f32[4096]{0:T(1024)S(1)}, u32[]{:S(2)}, u32[]{:S(2)}) collective-permute-start(f32[4096]{0:T(1024)S(1)} %bitcast.45), channel_id=1, source_target_pairs={{0,1},{1,0},{2,3},{3,2},{4,5},{5,4},{6,7},{7,6},{8,9},{9,8},{10,11... | collective-permute-start | bytes 49160 | tf_op jit(solution)/shard_map/ppermute | solution.py:13
  19.0 9.8 %collective-permute-start.18 = (f32[2048]{0:T(1024)S(1)}, f32[2048]{0:T(1024)S(1)}, u32[]{:S(2)}, u32[]{:S(2)}) collective-permute-start(f32[2048]{0:T(1024)S(1)} %maximum_select_fusion.11), channel_id=1, source_target_pairs={{0,8},{1,9},{2,10},{3,11},{4,12},{5,13},{6,14},{7,15},{8,0},{9,1},... | collective-permute-start | bytes 24584 | tf_op jit(solution)/shard_map/ppermute | solution.py:13
  32.2 19.1 %collective-permute-start.19 = (f32[4096]{0:T(1024)S(1)}, f32[4096]{0:T(1024)S(1)}, u32[]{:S(2)}, u32[]{:S(2)}) collective-permute-start(f32[4096]{0:T(1024)S(1)} %fusion.12), channel_id=1, source_target_pairs={{16,0},{17,1},{18,2},{19,3},{20,4},{21,5},{22,6},{23,7},{24,8},{25... | collective-permute-start | bytes 49160 | tf_op jit(solution)/shard_map/ppermute | solution.py:19
  34.0 17.3 %collective-permute-start.2 = (f32[4096]{0:T(1024)S(1)}, f32[4096]{0:T(1024)S(1)}, u32[]{:S(2)}, u32[]{:S(2)}) collective-permute-start(f32[4096]{0:T(1024)S(1)} %add.98), channel_id=1, source_target_pairs={{0,4},{1,5},{2,6},{3,7},{4,0},{5,1},{6,2},{7,3},{8,12},{9,13},{10,... | collective-permute-start | bytes 49160 | tf_op jit(solution)/shard_map/ppermute | solution.py:13
  51.3 12.3 %collective-permute-start.3 = (f32[4096]{0:T(1024)S(1)}, f32[4096]{0:T(1024)S(1)}, u32[]{:S(2)}, u32[]{:S(2)}) collective-permute-start(f32[4096]{0:T(1024)S(1)} %add.99), channel_id=1, source_target_pairs={{0,8},{1,9},{2,10},{3,11},{4,12},{5,13},{6,14},{7,15},{8,0},{9,1},... | collective-permute-start | bytes 49160 | tf_op jit(solution)/shard_map/ppermute | solution.py:13
  63.6 14.1 %collective-permute-start.20 = (f32[256]{0:T(256)S(1)}, f32[256]{0:T(256)S(1)}, u32[]{:S(2)}, u32[]{:S(2)}) collective-permute-start(f32[256]{0:T(256)S(1)} %bitcast.81), channel_id=1, source_target_pairs={{0,1},{1,0},{2,3},{3,2},{4,5},{5,4},{6,7},{7,6},{8,9},{9,8},{10,11... | collective-permute-start | bytes 3080 | tf_op jit(solution)/shard_map/ppermute | solution.py:13
  65.0 13.9 %collective-permute-start.4 = (f32[256]{0:T(256)S(1)}, f32[256]{0:T(256)S(1)}, u32[]{:S(2)}, u32[]{:S(2)}) collective-permute-start(f32[256]{0:T(256)S(1)} %dynamic-slice_multiply_fusion.5), channel_id=1, source_target_pairs={{0,16},{1,17},{2,18},{3,19},{4,20},{5,21},{6,22},{7,23},{8,24},{9,... | collective-permute-start | bytes 3080 | tf_op jit(solution)/shard_map/ppermute | solution.py:19
  77.6 6.0 %collective-permute-start.21 = (f32[512]{0:T(512)S(1)}, f32[512]{0:T(512)S(1)}, u32[]{:S(2)}, u32[]{:S(2)}) collective-permute-start(f32[512]{0:T(512)S(1)} %maximum_select_fusion.34), channel_id=1, source_target_pairs={{0,2},{1,3},{2,0},{3,1},{4,6},{5,7},{6,4},{7,5},{8,10},{9,11},{10,... | collective-permute-start | bytes 6152 | tf_op jit(solution)/shard_map/ppermute | solution.py:13
  84.8 12.4 %collective-permute-start.6 = (f32[4096]{0:T(1024)S(1)}, f32[4096]{0:T(1024)S(1)}, u32[]{:S(2)}, u32[]{:S(2)}) collective-permute-start(f32[4096]{0:T(1024)S(1)} %add.103), channel_id=1, source_target_pairs={{0,2},{1,3},{2,0},{3,1},{4,6},{5,7},{6,4},{7,5},{8,10},{9,11},{10,... | collective-permute-start | bytes 49160 | tf_op jit(solution)/shard_map/ppermute | solution.py:13
  88.3 7.6 %collective-permute-start.23 = (f32[2048]{0:T(1024)S(1)}, f32[2048]{0:T(1024)S(1)}, u32[]{:S(2)}, u32[]{:S(2)}) collective-permute-start(f32[2048]{0:T(1024)S(1)} %maximum_select_fusion.12), channel_id=1, source_target_pairs={{0,8},{1,9},{2,10},{3,11},{4,12},{5,13},{6,14},{7,15},{8,0},{9,1},... | collective-permute-start | bytes 24584 | tf_op jit(solution)/shard_map/ppermute | solution.py:13
  97.3 14.9 %collective-permute-start.24 = (f32[4096]{0:T(1024)S(1)}, f32[4096]{0:T(1024)S(1)}, u32[]{:S(2)}, u32[]{:S(2)}) collective-permute-start(f32[4096]{0:T(1024)S(1)} %fusion.10), channel_id=1, source_target_pairs={{16,0},{17,1},{18,2},{19,3},{20,4},{21,5},{22,6},{23,7},{24,8},{25... | collective-permute-start | bytes 49160 | tf_op jit(solution)/shard_map/ppermute | solution.py:19
  101.9 10.3 %collective-permute-start.8 = (f32[4096]{0:T(1024)S(1)}, f32[4096]{0:T(1024)S(1)}, u32[]{:S(2)}, u32[]{:S(2)}) collective-permute-start(f32[4096]{0:T(1024)S(1)} %add.105), channel_id=1, source_target_pairs={{0,8},{1,9},{2,10},{3,11},{4,12},{5,13},{6,14},{7,15},{8,0},{9,1},... | collective-permute-start | bytes 49160 | tf_op jit(solution)/shard_map/ppermute | solution.py:13
  113.6 18.9 %collective-permute-start.9 = (f32[256]{0:T(256)S(1)}, f32[256]{0:T(256)S(1)}, u32[]{:S(2)}, u32[]{:S(2)}) collective-permute-start(f32[256]{0:T(256)S(1)} %dynamic-slice_multiply_fusion.4), channel_id=1, source_target_pairs={{0,16},{1,17},{2,18},{3,19},{4,20},{5,21},{6,22},{7,23},{8,24},{9,... | collective-permute-start | bytes 3080 | tf_op jit(solution)/shard_map/ppermute | solution.py:19
  141.9 10.8 %collective-permute-start.12 = (f32[4096]{0:T(1024)S(1)}, f32[4096]{0:T(1024)S(1)}, u32[]{:S(2)}, u32[]{:S(2)}) collective-permute-start(f32[4096]{0:T(1024)S(1)} %add.108), channel_id=1, source_target_pairs={{0,4},{1,5},{2,6},{3,7},{4,0},{5,1},{6,2},{7,3},{8,12},{9,13},{10,... | collective-permute-start | bytes 49160 | tf_op jit(solution)/shard_map/ppermute | solution.py:13
  143.8 7.6 %collective-permute-start.28 = (f32[2048]{0:T(1024)S(1)}, f32[2048]{0:T(1024)S(1)}, u32[]{:S(2)}, u32[]{:S(2)}) collective-permute-start(f32[2048]{0:T(1024)S(1)} %maximum_select_fusion.13), channel_id=1, source_target_pairs={{0,8},{1,9},{2,10},{3,11},{4,12},{5,13},{6,14},{7,15},{8,0},{9,1},... | collective-permute-start | bytes 24584 | tf_op jit(solution)/shard_map/ppermute | solution.py:13
  152.7 7.8 %collective-permute-start.13 = (f32[4096]{0:T(1024)S(1)}, f32[4096]{0:T(1024)S(1)}, u32[]{:S(2)}, u32[]{:S(2)}) collective-permute-start(f32[4096]{0:T(1024)S(1)} %add.109), channel_id=1, source_target_pairs={{0,8},{1,9},{2,10},{3,11},{4,12},{5,13},{6,14},{7,15},{8,0},{9,1},... | collective-permute-start | bytes 49160 | tf_op jit(solution)/shard_map/ppermute | solution.py:13
  154.7 19.1 %collective-permute-start.29 = (f32[4096]{0:T(1024)S(1)}, f32[4096]{0:T(1024)S(1)}, u32[]{:S(2)}, u32[]{:S(2)}) collective-permute-start(f32[4096]{0:T(1024)S(1)} %fusion.8), channel_id=1, source_target_pairs={{16,0},{17,1},{18,2},{19,3},{20,4},{21,5},{22,6},{23,7},{24,8},{25... | collective-permute-start | bytes 49160 | tf_op jit(solution)/shard_map/ppermute | solution.py:19
  161.8 13.0 %collective-permute-start.14 = (f32[256]{0:T(256)S(1)}, f32[256]{0:T(256)S(1)}, u32[]{:S(2)}, u32[]{:S(2)}) collective-permute-start(f32[256]{0:T(256)S(1)} %dynamic-slice_multiply_fusion.3), channel_id=1, source_target_pairs={{0,16},{1,17},{2,18},{3,19},{4,20},{5,21},{6,22},{7,23},{8,24},{9,... | collective-permute-start | bytes 3080 | tf_op jit(solution)/shard_map/ppermute | solution.py:19
  189.0 6.1 %collective-permute-start.32 = (f32[1024]{0:T(1024)S(1)}, f32[1024]{0:T(1024)S(1)}, u32[]{:S(2)}, u32[]{:S(2)}) collective-permute-start(f32[1024]{0:T(1024)S(1)} %maximum_select_fusion.25), channel_id=1, source_target_pairs={{0,4},{1,5},{2,6},{3,7},{4,0},{5,1},{6,2},{7,3},{8,12},{9,13},{10,... | collective-permute-start | bytes 12296 | tf_op jit(solution)/shard_map/ppermute | solution.py:13
  192.2 12.2 %collective-permute-start.52 = (f32[4096]{0:T(1024)S(1)}, f32[4096]{0:T(1024)S(1)}, u32[]{:S(2)}, u32[]{:S(2)}) collective-permute-start(f32[4096]{0:T(1024)S(1)} %add.125), channel_id=1, source_target_pairs={{0,8},{1,9},{2,10},{3,11},{4,12},{5,13},{6,14},{7,15},{8,0},{9,1},... | collective-permute-start | bytes 49160 | tf_op jit(solution)/shard_map/ppermute | solution.py:13
  195.1 8.0 %collective-permute-start.33 = (f32[2048]{0:T(1024)S(1)}, f32[2048]{0:T(1024)S(1)}, u32[]{:S(2)}, u32[]{:S(2)}) collective-permute-start(f32[2048]{0:T(1024)S(1)} %maximum_select_fusion.14), channel_id=1, source_target_pairs={{0,8},{1,9},{2,10},{3,11},{4,12},{5,13},{6,14},{7,15},{8,0},{9,1},... | collective-permute-start | bytes 24584 | tf_op jit(solution)/shard_map/ppermute | solution.py:13
  214.6 5.5 %collective-permute-start.57 = (f32[256]{0:T(256)S(1)}, f32[256]{0:T(256)S(1)}, u32[]{:S(2)}, u32[]{:S(2)}) collective-permute-start(f32[256]{0:T(256)S(1)} %bitcast.72), channel_id=1, source_target_pairs={{0,1},{1,0},{2,3},{3,2},{4,5},{5,4},{6,7},{7,6},{8,9},{9,8},{10,11... | collective-permute-start | bytes 3080 | tf_op jit(solution)/shard_map/ppermute | solution.py:13
  215.7 11.0 %collective-permute-start.54 = (f32[512]{0:T(512)S(1)}, f32[512]{0:T(512)S(1)}, u32[]{:S(2)}, u32[]{:S(2)}) collective-permute-start(f32[512]{0:T(512)S(1)} %maximum_select_fusion.37), channel_id=1, source_target_pairs={{0,2},{1,3},{2,0},{3,1},{4,6},{5,7},{6,4},{7,5},{8,10},{9,11},{10,... | collective-permute-start | bytes 6152 | tf_op jit(solution)/shard_map/ppermute | solution.py:13
  220.1 25.5 %collective-permute-start.58 = (f32[512]{0:T(512)S(1)}, f32[512]{0:T(512)S(1)}, u32[]{:S(2)}, u32[]{:S(2)}) collective-permute-start(f32[512]{0:T(512)S(1)} %maximum_select_fusion.38), channel_id=1, source_target_pairs={{0,2},{1,3},{2,0},{3,1},{4,6},{5,7},{6,4},{7,5},{8,10},{9,11},{10,... | collective-permute-start | bytes 6152 | tf_op jit(solution)/shard_map/ppermute | solution.py:13
  223.7 7.7 %collective-permute-start.37 = (f32[4096]{0:T(1024)S(1)}, f32[4096]{0:T(1024)S(1)}, u32[]{:S(2)}, u32[]{:S(2)}) collective-permute-start(f32[4096]{0:T(1024)S(1)} %add.113), channel_id=1, source_target_pairs={{0,8},{1,9},{2,10},{3,11},{4,12},{5,13},{6,14},{7,15},{8,0},{9,1},... | collective-permute-start | bytes 49160 | tf_op jit(solution)/shard_map/ppermute | solution.py:13
  226.7 29.2 %collective-permute-start.55 = (f32[1024]{0:T(1024)S(1)}, f32[1024]{0:T(1024)S(1)}, u32[]{:S(2)}, u32[]{:S(2)}) collective-permute-start(f32[1024]{0:T(1024)S(1)} %maximum_select_fusion.26), channel_id=1, source_target_pairs={{0,4},{1,5},{2,6},{3,7},{4,0},{5,1},{6,2},{7,3},{8,12},{9,13},{10,... | collective-permute-start | bytes 12296 | tf_op jit(solution)/shard_map/ppermute | solution.py:13
  232.7 14.3 %collective-permute-start.38 = (f32[256]{0:T(256)S(1)}, f32[256]{0:T(256)S(1)}, u32[]{:S(2)}, u32[]{:S(2)}) collective-permute-start(f32[256]{0:T(256)S(1)} %dynamic-slice_multiply_fusion.2), channel_id=1, source_target_pairs={{0,16},{1,17},{2,18},{3,19},{4,20},{5,21},{6,22},{7,23},{8,24},{9,... | collective-permute-start | bytes 3080 | tf_op jit(solution)/shard_map/ppermute | solution.py:19
  245.7 6.1 %collective-permute-start.59 = (f32[1024]{0:T(1024)S(1)}, f32[1024]{0:T(1024)S(1)}, u32[]{:S(2)}, u32[]{:S(2)}) collective-permute-start(f32[1024]{0:T(1024)S(1)} %maximum_select_fusion.27), channel_id=1, source_target_pairs={{0,4},{1,5},{2,6},{3,7},{4,0},{5,1},{6,2},{7,3},{8,12},{9,13},{10,... | collective-permute-start | bytes 12296 | tf_op jit(solution)/shard_map/ppermute | solution.py:13
  251.8 7.7 %collective-permute-start.60 = (f32[2048]{0:T(1024)S(1)}, f32[2048]{0:T(1024)S(1)}, u32[]{:S(2)}, u32[]{:S(2)}) collective-permute-start(f32[2048]{0:T(1024)S(1)} %maximum_select_fusion.16), channel_id=1, source_target_pairs={{0,8},{1,9},{2,10},{3,11},{4,12},{5,13},{6,14},{7,15},{8,0},{9,1},... | collective-permute-start | bytes 24584 | tf_op jit(solution)/shard_map/ppermute | solution.py:13
  255.3 5.5 %collective-permute-start.40 = (f32[4096]{0:T(1024)S(1)}, f32[4096]{0:T(1024)S(1)}, u32[]{:S(2)}, u32[]{:S(2)}) collective-permute-start(f32[4096]{0:T(1024)S(1)} %add.115), channel_id=1, source_target_pairs={{0,2},{1,3},{2,0},{3,1},{4,6},{5,7},{6,4},{7,5},{8,10},{9,11},{10,... | collective-permute-start | bytes 49160 | tf_op jit(solution)/shard_map/ppermute | solution.py:13
  255.9 7.6 %collective-permute-start.56 = (f32[2048]{0:T(1024)S(1)}, f32[2048]{0:T(1024)S(1)}, u32[]{:S(2)}, u32[]{:S(2)}) collective-permute-start(f32[2048]{0:T(1024)S(1)} %maximum_select_fusion.15), channel_id=1, source_target_pairs={{0,8},{1,9},{2,10},{3,11},{4,12},{5,13},{6,14},{7,15},{8,0},{9,1},... | collective-permute-start | bytes 24584 | tf_op jit(solution)/shard_map/ppermute | solution.py:13
  263.5 14.4 %collective-permute-start.61 = (f32[4096]{0:T(1024)S(1)}, f32[4096]{0:T(1024)S(1)}, u32[]{:S(2)}, u32[]{:S(2)}) collective-permute-start(f32[4096]{0:T(1024)S(1)} %fusion.1), channel_id=1, source_target_pairs={{16,0},{17,1},{18,2},{19,3},{20,4},{21,5},{22,6},{23,7},{24,8},{25... | collective-permute-start | bytes 49160 | tf_op jit(solution)/shard_map/ppermute | solution.py:19
  265.6 12.3 %collective-permute-start.42 = (f32[4096]{0:T(1024)S(1)}, f32[4096]{0:T(1024)S(1)}, u32[]{:S(2)}, u32[]{:S(2)}) collective-permute-start(f32[4096]{0:T(1024)S(1)} %add.117), channel_id=1, source_target_pairs={{0,8},{1,9},{2,10},{3,11},{4,12},{5,13},{6,14},{7,15},{8,0},{9,1},... | collective-permute-start | bytes 49160 | tf_op jit(solution)/shard_map/ppermute | solution.py:13
  279.3 18.1 %collective-permute-start.43 = (f32[256]{0:T(256)S(1)}, f32[256]{0:T(256)S(1)}, u32[]{:S(2)}, u32[]{:S(2)}) collective-permute-start(f32[256]{0:T(256)S(1)} %dynamic-slice_multiply_fusion.1), channel_id=1, source_target_pairs={{0,16},{1,17},{2,18},{3,19},{4,20},{5,21},{6,22},{7,23},{8,24},{9,... | collective-permute-start | bytes 3080 | tf_op jit(solution)/shard_map/ppermute | solution.py:19
  307.0 7.6 %collective-permute-start.69 = (f32[2048]{0:T(1024)S(1)}, f32[2048]{0:T(1024)S(1)}, u32[]{:S(2)}, u32[]{:S(2)}) collective-permute-start(f32[2048]{0:T(1024)S(1)} %maximum_select_fusion.18), channel_id=1, source_target_pairs={{0,8},{1,9},{2,10},{3,11},{4,12},{5,13},{6,14},{7,15},{8,0},{9,1},... | collective-permute-start | bytes 24584 | tf_op jit(solution)/shard_map/ppermute | solution.py:13
  309.7 7.6 %collective-permute-start.65 = (f32[2048]{0:T(1024)S(1)}, f32[2048]{0:T(1024)S(1)}, u32[]{:S(2)}, u32[]{:S(2)}) collective-permute-start(f32[2048]{0:T(1024)S(1)} %maximum_select_fusion.17), channel_id=1, source_target_pairs={{0,8},{1,9},{2,10},{3,11},{4,12},{5,13},{6,14},{7,15},{8,0},{9,1},... | collective-permute-start | bytes 24584 | tf_op jit(solution)/shard_map/ppermute | solution.py:13
  317.3 14.5 %collective-permute-start.70 = (f32[4096]{0:T(1024)S(1)}, f32[4096]{0:T(1024)S(1)}, u32[]{:S(2)}, u32[]{:S(2)}) collective-permute-start(f32[4096]{0:T(1024)S(1)} %fusion.3), channel_id=1, source_target_pairs={{16,0},{17,1},{18,2},{19,3},{20,4},{21,5},{22,6},{23,7},{24,8},{25... | collective-permute-start | bytes 49160 | tf_op jit(solution)/shard_map/ppermute | solution.py:19
  344.1 6.5 %collective-permute-start.73 = (f32[1024]{0:T(1024)S(1)}, f32[1024]{0:T(1024)S(1)}, u32[]{:S(2)}, u32[]{:S(2)}) collective-permute-start(f32[1024]{0:T(1024)S(1)} %maximum_select_fusion.30), channel_id=1, source_target_pairs={{0,4},{1,5},{2,6},{3,7},{4,0},{5,1},{6,2},{7,3},{8,12},{9,13},{10,... | collective-permute-start | bytes 12296 | tf_op jit(solution)/shard_map/ppermute | solution.py:13
  346.8 8.8 %collective-permute-start.78 = (f32[2048]{0:T(1024)S(1)}, f32[2048]{0:T(1024)S(1)}, u32[]{:S(2)}, u32[]{:S(2)}) collective-permute-start(f32[2048]{0:T(1024)S(1)} %maximum_select_fusion.20), channel_id=1, source_target_pairs={{0,8},{1,9},{2,10},{3,11},{4,12},{5,13},{6,14},{7,15},{8,0},{9,1},... | collective-permute-start | bytes 24584 | tf_op jit(solution)/shard_map/ppermute | solution.py:13
  350.6 7.6 %collective-permute-start.74 = (f32[2048]{0:T(1024)S(1)}, f32[2048]{0:T(1024)S(1)}, u32[]{:S(2)}, u32[]{:S(2)}) collective-permute-start(f32[2048]{0:T(1024)S(1)} %maximum_select_fusion.19), channel_id=1, source_target_pairs={{0,8},{1,9},{2,10},{3,11},{4,12},{5,13},{6,14},{7,15},{8,0},{9,1},... | collective-permute-start | bytes 24584 | tf_op jit(solution)/shard_map/ppermute | solution.py:13
  358.2 14.5 %collective-permute-start.79 = (f32[4096]{0:T(1024)S(1)}, f32[4096]{0:T(1024)S(1)}, u32[]{:S(2)}, u32[]{:S(2)}) collective-permute-start(f32[4096]{0:T(1024)S(1)} %fusion.5), channel_id=1, source_target_pairs={{16,0},{17,1},{18,2},{19,3},{20,4},{21,5},{22,6},{23,7},{24,8},{25... | collective-permute-start | bytes 49160 | tf_op jit(solution)/shard_map/ppermute | solution.py:19
  359.5 19.0 %collective-permute-start.45 = (f32[4096]{0:T(1024)S(1)}, f32[4096]{0:T(1024)S(1)}, u32[]{:S(2)}, u32[]{:S(2)}) collective-permute-start(f32[4096]{0:T(1024)S(1)} %add.119), channel_id=1, source_target_pairs={{0,2},{1,3},{2,0},{3,1},{4,6},{5,7},{6,4},{7,5},{8,10},{9,11},{10,... | collective-permute-start | bytes 49160 | tf_op jit(solution)/shard_map/ppermute | solution.py:13
  379.6 6.1 %collective-permute-start.81 = (f32[512]{0:T(512)S(1)}, f32[512]{0:T(512)S(1)}, u32[]{:S(2)}, u32[]{:S(2)}) collective-permute-start(f32[512]{0:T(512)S(1)} %maximum_select_fusion.43), channel_id=1, source_target_pairs={{0,2},{1,3},{2,0},{3,1},{4,6},{5,7},{6,4},{7,5},{8,10},{9,11},{10,... | collective-permute-start | bytes 6152 | tf_op jit(solution)/shard_map/ppermute | solution.py:13
  383.3 8.0 %collective-permute-start.47 = (f32[4096]{0:T(1024)S(1)}, f32[4096]{0:T(1024)S(1)}, u32[]{:S(2)}, u32[]{:S(2)}) collective-permute-start(f32[4096]{0:T(1024)S(1)} %add.121), channel_id=1, source_target_pairs={{0,8},{1,9},{2,10},{3,11},{4,12},{5,13},{6,14},{7,15},{8,0},{9,1},... | collective-permute-start | bytes 49160 | tf_op jit(solution)/shard_map/ppermute | solution.py:13
  385.7 6.8 %collective-permute-start.82 = (f32[1024]{0:T(1024)S(1)}, f32[1024]{0:T(1024)S(1)}, u32[]{:S(2)}, u32[]{:S(2)}) collective-permute-start(f32[1024]{0:T(1024)S(1)} %maximum_select_fusion.32), channel_id=1, source_target_pairs={{0,4},{1,5},{2,6},{3,7},{4,0},{5,1},{6,2},{7,3},{8,12},{9,13},{10,... | collective-permute-start | bytes 12296 | tf_op jit(solution)/shard_map/ppermute | solution.py:13
  392.6 11.8 %collective-permute-start.83 = (f32[2048]{0:T(1024)S(1)}, f32[2048]{0:T(1024)S(1)}, u32[]{:S(2)}, u32[]{:S(2)}) collective-permute-start(f32[2048]{0:T(1024)S(1)} %maximum_select_fusion.21), channel_id=1, source_target_pairs={{0,8},{1,9},{2,10},{3,11},{4,12},{5,13},{6,14},{7,15},{8,0},{9,1},... | collective-permute-start | bytes 24584 | tf_op jit(solution)/shard_map/ppermute | solution.py:13
  394.9 10.8 %collective-permute-start.48 = (f32[256]{0:T(256)S(1)}, f32[256]{0:T(256)S(1)}, u32[]{:S(2)}, u32[]{:S(2)}) collective-permute-start(f32[256]{0:T(256)S(1)} %dynamic-slice_multiply_fusion), channel_id=1, source_target_pairs={{0,16},{1,17},{2,18},{3,19},{4,20},{5,21},{6,22},{7,23},{8,24},{9,... | collective-permute-start | bytes 3080 | tf_op jit(solution)/shard_map/ppermute | solution.py:19
  (42 other events, 266.2 us)
where the time goes:
time: 415 us; the launch traced here: 407 us
  starting transfers between devices  188 us (45%)
  waiting for transfers between devices  127 us (31%)
  matrix products  69.4 us (17%)
  between operations  11.5 us (3%)
  other arithmetic  10.5 us (3%)
    ppermute x72, starting transfers between devices, swapped(): lax.ppermute(value, axis, [(i, i ^ 1 << apart) for i in range(lax.axis_si...  108 us
    ppermute x12, starting transfers between devices, from_behind(): return lax.ppermute(block, axis, route)  80.2 us
    ppermute x72, waiting for transfers between devices, swapped(): lax.ppermute(value, axis, [(i, i ^ 1 << apart) for i in range(lax.axis_si...  66.1 us
    ppermute x12, waiting for transfers between devices, from_behind(): return lax.ppermute(block, axis, route)  60.7 us
    dot_general x8, matrix products, on_device(): jnp.dot(kernel, backward_state[1], precision=lax.Precision.HIGHEST, prefe...  43.5 us
    dot_general x7, matrix products, on_device(): jnp.dot(forward_state[1], kernel, precision=lax.Precision.HIGHEST, prefer...  25.9 us
  transfers between devices with their start and end apart: 84, of which 45 were waited for; matrix products, arithmetic and copies ran while one was open for 13% of the time, Pallas kernels for 0%

commit v1 on v0

v1 whole, which is shorter than its diff:
```python
import functools
import math

import jax
import jax.numpy as jnp
from jax import lax
from jax.experimental import pallas as pl
from jax.experimental.pallas import tpu as pltpu
from jax.sharding import PartitionSpec as P

ENTROPIC = 0.25
LANES = 128
SUBLANES = 8
CHUNKS = 8
OWNERS = 2
MESH = pl.DeviceIdType.MESH


def eye():
    shape = (LANES, LANES)
    return lax.broadcasted_iota(jnp.int32, shape, 0) == lax.broadcasted_iota(jnp.int32, shape, 1)


def total(x):
    return jnp.sum(jnp.sum(x, axis=0, keepdims=True), axis=1, keepdims=True)


def chain_kernel(
    width, kernels, cost, marginals, final, out,
    kernel, column, row_sums, marg, fin, alpha, beta, scaling, w0,
    rs_out, rs_in, ag_out, col_in, f0_out, f0_in, f1_out, f1_in, b0_out, b0_in, w1_out, w1_in, ar_in, ls_out, ls_sent,
    load_sem, send_sem, recv_sem,
):
    rows, states = kernel.shape
    blocks = states // LANES
    piece = rows // LANES
    half = width // OWNERS
    me = lax.axis_index("chain")
    g = me // width
    m = me % width
    start = g * width
    last = g == kernels - 1

    def copy(src, dst, slot, target):
        return pltpu.make_async_remote_copy(
            src_ref=src, dst_ref=dst, send_sem=send_sem.at[slot], recv_sem=recv_sem.at[slot],
            device_id={"chain": target}, device_id_type=MESH,
        )

    def received(ref, slot):
        copy(ref, ref, slot, me).wait_recv()

    def sent(ref, slot):
        copy(ref, ref, slot, me).wait_send()

    barrier = pltpu.get_barrier_semaphore()

    def greet(target):
        pl.semaphore_signal(barrier, inc=1, device_id={"chain": target}, device_id_type=MESH)

    @pl.loop(0, width)
    def _(i):
        @pl.when(i != m)
        def _():
            greet(start + i)

        @pl.when(g > 0)
        def _():
            greet(start - width + i)

        @pl.when(g < kernels - 1)
        def _():
            greet(start + width + i)

    span = rows // CHUNKS

    def load(c):
        part = pl.ds(c * span, span)
        return pltpu.make_async_copy(cost.at[part], kernel.at[part], load_sem.at[c])

    for c in range(CHUNKS):
        load(c).start()
    marg_load = pltpu.make_async_copy(marginals, marg, load_sem.at[CHUNKS])
    fin_load = pltpu.make_async_copy(final, fin, load_sem.at[CHUNKS + 1])
    marg_load.start()
    fin_load.start()

    lane = [slice(b * LANES, (b + 1) * LANES) for b in range(blocks)]

    def row_of_column(ref):
        parts = []
        for h in range(piece):
            x = ref[h * LANES : (h + 1) * LANES, :]
            parts.append(jnp.sum(jnp.where(eye(), x, 0.0), axis=0, keepdims=True))
        return jnp.concatenate(parts, axis=0)

    def column_of_row(value):
        for h in range(piece):
            x = jnp.broadcast_to(value[h : h + 1, :], (LANES, LANES))
            x = jnp.sum(jnp.where(eye(), x, 0.0), axis=1, keepdims=True)
            column[h * LANES : (h + 1) * LANES, :] = jnp.broadcast_to(x, (LANES, LANES))

    def tree(values):
        while len(values) > 1:
            values = [a + b for a, b in zip(values[::2], values[1::2])] + values[len(values) // 2 * 2 :]
        return values[0]

    def put_pieces(acc, ref):
        whole = []
        for i in range(width):
            rows_of = [jnp.sum(acc[i * piece + h], axis=0, keepdims=True) for h in range(piece)]
            whole += rows_of
            for h in range(piece):
                ref[i, h : h + 1, :] = rows_of[h]
        whole = tree(whole)
        for i in range(width):
            ref[i, piece : piece + 1, :] = whole

    def sum_pieces(ref):
        x = tree([ref[i] for i in range(width)])
        return x[:piece], total(x[piece:])

    def forward(ref):
        def step(r, acc):
            at = pl.ds(pl.multiple_of(r * SUBLANES, SUBLANES), SUBLANES)
            v = column[at, :]
            return tuple(a + kernel[at, l] * v for a, l in zip(acc, lane))

        zero = tuple(jnp.zeros((SUBLANES, LANES), jnp.float32) for _ in lane)
        put_pieces(lax.fori_loop(0, rows // SUBLANES, step, zero, unroll=2), ref)

    def backward(w):
        ws = [jnp.broadcast_to(w(b), (SUBLANES, LANES)) for b in range(blocks)]

        def step(r, carry):
            at = pl.ds(pl.multiple_of(r * SUBLANES, SUBLANES), SUBLANES)
            x = tree([tree([kernel[at, lane[b]] * ws[b] for b in range(q, q + 8)]) for q in range(0, blocks, 8)])
            column[at, :] = jnp.broadcast_to(jnp.sum(x, axis=1, keepdims=True), (SUBLANES, LANES))
            return carry

        lax.fori_loop(0, rows // SUBLANES, step, 0, unroll=2)
        return row_of_column(column)

    rate = -math.log2(math.e) / ENTROPIC

    def chunk_step(r, acc):
        at = pl.ds(pl.multiple_of(r * SUBLANES, SUBLANES), SUBLANES)
        new = []
        xs = []
        for a, l in zip(acc, lane):
            x = jnp.exp2(kernel[at, l] * rate)
            kernel[at, l] = x
            xs.append(x)
            new.append(a + x)
        x = tree(xs)
        row_sums[at, :] = jnp.broadcast_to(jnp.sum(x, axis=1, keepdims=True), (SUBLANES, LANES))
        return tuple(new)

    acc = tuple(jnp.zeros((SUBLANES, LANES), jnp.float32) for _ in lane)
    for c in range(CHUNKS):
        load(c).wait()
        acc = lax.fori_loop(c * span // SUBLANES, (c + 1) * span // SUBLANES, chunk_step, acc)
    put_pieces(acc, rs_out)

    greeted = width - 1 + width * ((g > 0).astype(jnp.int32) + (g < kernels - 1).astype(jnp.int32))
    pl.semaphore_wait(barrier, greeted)

    RS, AG, F0, F1, B0, W1, AR, LS = range(8)

    def to_group(src, dst, slot, group, first):
        @pl.loop(0, width)
        def _(j):
            i = width - 1 - j if first == "high" else j
            copy(src(i), dst.at[m], slot, group * width + i).start()

    def to_own(src, dst, slot):
        @pl.loop(1, width)
        def _(j):
            i = (m + j) % width
            copy(src(i), dst.at[m], slot, start + i).start()

    @pl.when(g == 0)
    def _():
        to_group(lambda i: rs_out.at[i], f0_in, F0, g + 1, "high")

    @pl.when(last)
    def _():
        b = row_of_column(row_sums)
        beta[...] = b
        b0_out[0:piece, :] = b
        b0_out[piece : piece + 1, :] = jnp.sum(b, axis=0, keepdims=True)
        to_group(lambda i: b0_out, b0_in, B0, g - 1, "low")

    to_own(lambda i: rs_out.at[i], rs_in, RS)
    rs_in[m] = rs_out[m]
    received(rs_in.at[pl.ds(0, width - 1)], RS)
    block, _ = sum_pieces(rs_in)
    ag_out[...] = block
    col_in[m] = block
    to_own(lambda i: ag_out, col_in, AG)

    marg_load.wait()
    fin_load.wait()
    scaling[...] = jnp.ones_like(scaling)
    alpha[...] = jnp.ones_like(alpha)

    def forward_0():
        received(f0_in, F0)
        a, s = sum_pieces(f0_in)
        a = a * (states / s)
        alpha[...] = a
        column_of_row(a)
        forward(f0_out)

    def set_beta(b, w):
        s = total(jnp.sum(col_in[...] * w, axis=0))
        beta[...] = b * (states / s)

    @pl.when(g == 1)
    def _():
        forward_0()
        to_group(lambda i: f0_out.at[i], f0_in, F0, g + 1, "high")

    received(col_in.at[pl.ds(0, width - 1)], AG)

    @pl.when(jnp.logical_not(last))
    def _():
        received(b0_in, B0)
        x = b0_in[...]
        s = total(tree([x[i, piece:] for i in range(width)]))
        w = x[:, :piece] * (states / s)
        w0[...] = w
        b = backward(lambda k: w0[k // piece, k % piece : k % piece + 1, :])

        @pl.when(g > 0)
        def _():
            b0_out[0:piece, :] = b
            b0_out[piece : piece + 1, :] = jnp.sum(b, axis=0, keepdims=True)
            to_group(lambda i: b0_out, b0_in, B0, g - 1, "low")

        set_beta(b, w)

    @pl.when(last)
    def _():
        set_beta(beta[...], jnp.ones((width, piece, LANES), jnp.float32))

    @pl.when(g > 1)
    def _():
        forward_0()

    @pl.when(jnp.logical_and(g > 1, jnp.logical_not(last)))
    def _():
        to_group(lambda i: f0_out.at[i], f0_in, F0, g + 1, "high")

    @pl.when(last)
    def _():
        for o in range(OWNERS):
            part = pl.ds(o * half, half)
            owner = width - OWNERS + o

            @pl.when(m != owner)
            def _():
                copy(f0_out.at[part], ar_in.at[m], AR, start + owner).start()

        for o in range(OWNERS):
            part = pl.ds(o * half, half)
            owner = width - OWNERS + o

            @pl.when(m == owner)
            def _():
                ar_in[m] = f0_out[part]
                received(ar_in.at[pl.ds(0, width - 1)], AR)
                x = tree([ar_in[i] for i in range(width)])
                s = total(x[0, piece:])
                ls = fin[part] / (x[:, :piece] * (states / s))
                ls_out[...] = ls
                w1_in[part] = ls

                @pl.loop(0, width)
                def _(i):
                    @pl.when(i != owner)
                    def _():
                        copy(ls_out, w1_in.at[part], LS, start + i).start()

                for other in range(OWNERS):
                    if other != o:
                        received(w1_in.at[pl.ds(other * half, half)], LS)

        @pl.when(m < width - OWNERS)
        def _():
            received(w1_in, LS)

    scaling[...] = marg[...] / (alpha[...] * beta[...])

    def backward_1():
        w = w1_in[...]
        b = backward(lambda k: w1_in[k // piece, k % piece : k % piece + 1, :])
        set_beta(b, w)

        @pl.when(g > 0)
        def _():
            w1_out[...] = scaling[...] * beta[...]
            to_group(lambda i: w1_out, w1_in, W1, g - 1, "low")

    @pl.when(last)
    def _():
        backward_1()

    @pl.when(g > 0)
    def _():
        received(f1_in, F1)
        a, s = sum_pieces(f1_in)
        alpha[...] = a * (states / s)

    @pl.when(jnp.logical_not(last))
    def _():
        column_of_row(scaling[...] * alpha[...])
        forward(f1_out)
        to_group(lambda i: f1_out.at[i], f1_in, F1, g + 1, "high")
        received(w1_in, W1)
        backward_1()

    out[...] = marg[...] / (alpha[...] * beta[...])

    sent(rs_in.at[pl.ds(0, width - 1)], RS)
    sent(col_in.at[pl.ds(0, width - 1)], AG)

    @pl.when(jnp.logical_not(last))
    def _():
        sent(f0_in, F0)
        sent(f1_in, F1)

    @pl.when(g > 0)
    def _():
        sent(b0_in, B0)
        sent(w1_in, W1)

    @pl.when(last)
    def _():
        for o in range(OWNERS):
            owner = width - OWNERS + o

            @pl.when(m != owner)
            def _():
                sent(ar_in.at[m], AR)

            @pl.when(m == owner)
            def _():
                sent(ls_sent, LS)


def solution(mesh):
    chain = mesh.shape["chain"]

    def on_device(cost, marginals, final_marginal):
        rows, states = cost.shape
        width = states // rows
        piece = rows // LANES

        def buffer(*shape):
            return pltpu.VMEM(shape + (LANES,), jnp.float32)

        pieces = buffer(width, piece + 1)
        whole = buffer(width, piece)
        one = buffer(piece)
        half = width // OWNERS
        scratch = [
            pltpu.VMEM((rows, states), jnp.float32), buffer(rows), buffer(rows),
            one, whole, one, one, one, whole,
            pieces, pieces, one, whole, pieces, pieces, pieces, pieces, buffer(piece + 1), pieces, one, whole,
            buffer(width, half, piece + 1), buffer(half, piece), buffer(width - 1, half, piece),
            pltpu.SemaphoreType.DMA((CHUNKS + 2,)), pltpu.SemaphoreType.DMA((8,)), pltpu.SemaphoreType.DMA((8,)),
        ]
        scaling = pl.pallas_call(
            functools.partial(chain_kernel, width, chain // width),
            out_shape=jax.ShapeDtypeStruct((piece, LANES), jnp.float32),
            in_specs=[pl.BlockSpec(memory_space=pl.ANY)] * 3,
            out_specs=pl.BlockSpec(memory_space=pltpu.VMEM),
            scratch_shapes=scratch,
            compiler_params=pltpu.CompilerParams(collective_id=0, has_side_effects=True),
            name="sinkhorn_chain",
        )(cost, marginals.reshape(piece, LANES), final_marginal.reshape(width, piece, LANES))
        return jnp.log(scaling).reshape(rows)

    placed = (P(("pop", "chain"), None), P(("pop", "chain")), P("pop"))
    return jax.shard_map(on_device, mesh=mesh, in_specs=placed, out_specs=P(("pop", "chain")), check_vma=False)
```

time: 415 us -> 118 us (0.28)
  the two profiles are of different devices: /device:TPU:44 before, /device:TPU:37 now
where the time goes in v1:
time: 118 us
  Pallas kernels  117 us (99%)
  local copies, waits for them, and re-layouts  1.25 us (1%)
    pallas_call x1, Pallas kernels, on_device(): pl.pallas_call(functools.partial(chain_kernel, width, chain // width), ou...  117 us

profile of v1, /device:TPU:37, one launch (start us, length us, event | category | flops | bytes accessed | tf_op | source)
XLA Modules:
  0.0 118.2 jit_solution(1628035405895537264)
XLA Ops:
  0.0 117.0 %sinkhorn_chain.1 = f32[2,128]{1,0:T(2,128)} custom-call(f32[256,4096]{1,0:T(8,128)} %cost.1, f32[2,128]{1,0:T(2,128)} %bitcast.5, f32[16,2,128]{2,1,0:T(2,128)} %bitcast.4), custom_call_target="tpu_custom_call" | custom-call | tf_op jit(solution)/shard_map/sinkhorn_chain/pallas_call | solution.py:374
  117.0 1.2 %log_bitcast_fusion = f32[256]{0:T(256)} fusion(f32[2,128]{1,0:T(2,128)} %sinkhorn_chain.1), kind=kLoop, calls=%fused_computation | loop fusion | bytes 2048 | tf_op jit(solution)/shard_map/reshape | solution.py:383

commit v2 on v0

v2 whole, which is shorter than its diff:
```python
import functools
import math

import jax
import jax.numpy as jnp
from jax import lax
from jax.experimental import pallas as pl
from jax.experimental.pallas import tpu as pltpu
from jax.sharding import PartitionSpec as P

ENTROPIC = 0.25
LANES = 128
SUBLANES = 8
CHUNKS = 8
CORES = 2
QUARTERS = 4
MESH = pl.DeviceIdType.MESH
SLOTS = range(17)
KX, PK, RX, MX, CS, CB, A1, F0, AR, LS, B0, W1, F1, AX, BX, AO, BO = SLOTS


def eye():
    shape = (LANES, LANES)
    return lax.broadcasted_iota(jnp.int32, shape, 0) == lax.broadcasted_iota(jnp.int32, shape, 1)


def total(x):
    return jnp.sum(jnp.sum(x, axis=0, keepdims=True), axis=1, keepdims=True)


def tree(values):
    while len(values) > 1:
        values = [a + b for a, b in zip(values[::2], values[1::2])] + values[len(values) // 2 * 2 :]
    return values[0]


def signal(sem, target):
    pl.semaphore_signal(sem, inc=1, device_id={"chain": target}, device_id_type=MESH)


def chain_kernel(
    width, kernels, cost, marginals, final, out,
    kernel, column, marg, fin, row_out, row_in, rsum, col_out, col_mate, col_in, cs_in, many,
    a1_in, f_out, f0_in, f1_in, ar_in, b0_out, b0_in, w0, w1_out, w1_in,
    alpha, alpha_in, beta, beta_in, alpha_last, beta_last,
    load_sem, send_sem, recv_sem, token,
):
    states = kernel.shape[1]
    rows = kernel.shape[0] // CORES
    blocks = states // LANES
    piece = kernel.shape[0] // LANES
    chips = width // CORES
    me = lax.axis_index("chain")
    g = me // width
    m = me % width
    chip = m // CORES
    core = m % CORES
    mate = me + 1 - 2 * core
    start = g * width
    first_g, last_g = g == 0, g == kernels - 1
    lead = core == 1
    up_collector = jnp.logical_and(lead, chip == chips - 1)
    down_collector = jnp.logical_and(lead, chip == 0)
    owner = start + width - 1

    def when(condition):
        return pl.when(condition)

    def both(*conditions):
        return functools.reduce(jnp.logical_and, conditions)

    def no(condition):
        return jnp.logical_not(condition)

    def copy(src, dst, slot, target):
        return pltpu.make_async_remote_copy(
            src_ref=src, dst_ref=dst, send_sem=send_sem.at[slot], recv_sem=recv_sem.at[slot],
            device_id={"chain": target}, device_id_type=MESH,
        )

    def received(ref, slot):
        copy(ref, ref, slot, mate).wait_recv()

    def sent(ref, slot):
        copy(ref, ref, slot, mate).wait_send()

    barrier = pltpu.get_barrier_semaphore()
    signal(barrier, mate)

    @when(both(me != owner, mate != owner))
    def _():
        signal(barrier, owner)

    @when(both(me != start + 1, mate != start + 1))
    def _():
        signal(barrier, start + 1)

    @when(no(first_g))
    def _():
        signal(barrier, owner - width)

    @when(no(last_g))
    def _():
        signal(barrier, start + width + 1)

    @when(up_collector)
    def _():
        for i in range(1, chips - 1):
            signal(barrier, start + CORES * i + 1)

    span = rows // CHUNKS
    base = core * rows

    def load(c):
        return pltpu.make_async_copy(
            cost.at[pl.ds(c * span, span)], kernel.at[pl.ds(base + c * span, span)], load_sem.at[c]
        )

    for c in range(CHUNKS):
        load(c).start()
    marg_load = pltpu.make_async_copy(marginals, marg.at[core], load_sem.at[CHUNKS])
    fin_load = pltpu.make_async_copy(final, fin, load_sem.at[CHUNKS + 1])
    marg_load.start()
    fin_load.start()

    def lanes(b):
        return slice(b * LANES, (b + 1) * LANES)

    def row_of_column(ref, count):
        parts = []
        for h in range(count):
            x = ref[h * LANES : (h + 1) * LANES, :]
            parts.append(jnp.sum(jnp.where(eye(), x, 0.0), axis=0, keepdims=True))
        return jnp.concatenate(parts, axis=0)

    def column_of_row(value):
        for h in range(piece):
            x = jnp.broadcast_to(value[h : h + 1, :], (LANES, LANES))
            x = jnp.sum(jnp.where(eye(), x, 0.0), axis=1, keepdims=True)
            column[h * LANES : (h + 1) * LANES, :] = jnp.broadcast_to(x, (LANES, LANES))

    def forward(v, order, send):
        column_of_row(v)
        row = jnp.sum(v * rsum[...], axis=0, keepdims=True)
        quarters = min(QUARTERS, chips)
        for q in range(quarters):
            targets = order[q * chips // quarters : (q + 1) * chips // quarters]
            mine = [i * piece + h for i in targets for h in range(piece)]

            def step(r, acc):
                at = pl.ds(pl.multiple_of(r * SUBLANES, SUBLANES), SUBLANES)
                v = column[at, :]
                return tuple(a + kernel[at, lanes(b)] * v for a, b in zip(acc, mine))

            zero = tuple(jnp.zeros((SUBLANES, LANES), jnp.float32) for _ in mine)
            acc = lax.fori_loop(0, CORES * rows // SUBLANES, step, zero, unroll=8)
            for n, i in enumerate(targets):
                for h in range(piece):
                    f_out[i, h : h + 1, :] = jnp.sum(acc[n * piece + h], axis=0, keepdims=True)
                f_out[i, piece : piece + 1, :] = row
            for i in targets:
                send(i)

    def backward(ref):
        ws = [
            jnp.broadcast_to(ref[b // piece, b % piece : b % piece + 1, :], (SUBLANES, LANES)) for b in range(blocks)
        ]

        def step(r, carry):
            at = pl.ds(pl.multiple_of(r * SUBLANES, SUBLANES), SUBLANES)
            x = tree([tree([kernel[at, lanes(b)] * ws[b] for b in range(q, q + 8)]) for q in range(0, blocks, 8)])
            column[at, :] = jnp.broadcast_to(jnp.sum(x, axis=1, keepdims=True), (SUBLANES, LANES))
            return carry

        lax.fori_loop(0, CORES * rows // SUBLANES, step, 0, unroll=4)
        return row_of_column(column, piece)

    def sum_pieces(ref):
        x = tree([ref[i] for i in range(chips)])
        return x[:piece], total(x[piece:])

    rate = -math.log2(math.e) / ENTROPIC

    def chunk_step(r, acc):
        at = pl.ds(pl.multiple_of(base + r * SUBLANES, SUBLANES), SUBLANES)
        new, xs = [], []
        for b in range(blocks):
            x = jnp.exp2(kernel[at, lanes(b)] * rate)
            kernel[at, lanes(b)] = x
            xs.append(x)
            new.append(acc[b] + x)
        here = pl.ds(pl.multiple_of(r * SUBLANES, SUBLANES), SUBLANES)
        column[here, :] = jnp.broadcast_to(jnp.sum(tree(xs), axis=1, keepdims=True), (SUBLANES, LANES))
        return tuple(new)

    acc = tuple(jnp.zeros((SUBLANES, LANES), jnp.float32) for _ in range(blocks))
    for c in range(CHUNKS):
        load(c).wait()
        acc = lax.fori_loop(c * span // SUBLANES, (c + 1) * span // SUBLANES, chunk_step, acc)
    for b in range(blocks):
        col_out[b // piece, b % piece : b % piece + 1, :] = jnp.sum(acc[b], axis=0, keepdims=True)
    row_out[...] = row_of_column(column, piece // CORES)
    marg_load.wait()
    fin_load.wait()

    greeted = jnp.where(lead, 2, 1)
    greeted = jnp.where(down_collector, width - 1 + jnp.where(first_g, 0, width), greeted)
    greeted = jnp.where(up_collector, width - 1 + jnp.where(last_g, 0, width), greeted)
    pl.semaphore_wait(barrier, greeted)

    @when(no(lead))
    def _():
        copy(col_out, col_mate, PK, mate).start()

    copy(row_out, row_in, RX, mate).start()
    copy(marg.at[core], marg.at[core], MX, mate).start()
    half = kernel.at[pl.ds(base, rows)]
    copy(half, half, KX, mate).start()

    UP, DOWN = 0, 1

    @when(both(up_collector, no(last_g)))
    def _():
        for i in range(width - 1):
            signal(token.at[UP], start + i)

    @when(both(down_collector, no(first_g)))
    def _():
        for i in range(width):
            if i != 1:
                signal(token.at[DOWN], start + i)

    def wait_up():
        @when(both(no(up_collector), no(last_g)))
        def _():
            pl.semaphore_wait(token.at[UP], 1)

    def wait_down():
        @when(both(no(down_collector), no(first_g)))
        def _():
            pl.semaphore_wait(token.at[DOWN], 1)

    def to_group(src, dst, slot, group, i):
        copy(src, dst.at[chip], slot, group * width + CORES * i + core).start()

    high = list(range(chips - 1, -1, -1))
    low = list(range(chips))

    @when(lead)
    def _():
        received(col_mate, PK)
        col_out[...] = col_out[...] + col_mate[...]

    @when(both(lead, no(up_collector)))
    def _():
        copy(col_out, cs_in.at[chip], CS, owner).start()

    @when(up_collector)
    def _():
        cs_in[chips - 1] = col_out[...]
        received(cs_in.at[pl.ds(0, chips - 1)], CS)
        c = tree([cs_in[i] for i in range(chips)])
        col_in[...] = c

        @when(first_g)
        def _():
            w1_out[...] = c * (states / total(jnp.sum(c, axis=0)))
            for i in high:
                copy(w1_out.at[i], a1_in, A1, start + width + CORES * i + 1).start()

        for i in range(width - 1):
            copy(col_in, col_in, CB, start + i).start()

    received(row_in, RX)

    @when(lead)
    def _():
        rsum[...] = jnp.concatenate([row_in[...], row_out[...]], axis=0)

    @when(no(lead))
    def _():
        rsum[...] = jnp.concatenate([row_out[...], row_in[...]], axis=0)

    received(marg.at[1 - core], MX)
    target = jnp.concatenate([marg[i] for i in range(CORES)], axis=0)

    def set_beta(ref, b, w):
        s = total(jnp.sum(col_in[...] * w, axis=0))
        ref[...] = b * (states / s)

    @when(lead)
    def _():
        alpha[...] = jnp.ones_like(alpha)

        @when(g == 1)
        def _():
            received(a1_in, A1)
            alpha[...] = a1_in[...]

        @when(g > 1)
        def _():
            received(f0_in, F0)
            a, s = sum_pieces(f0_in)
            alpha[...] = a * (states / s)

        received(kernel.at[pl.ds(0, rows)], KX)
        wait_up()

        @when(no(first_g))
        def _():
            def send(i):
                @when(no(last_g))
                def _():
                    to_group(f_out.at[i], f0_in, F0, g + 1, i)

            forward(alpha[...], high, send)
            copy(alpha, alpha_in, AX, mate).start()

        @when(both(last_g, no(up_collector)))
        def _():
            copy(f_out, ar_in.at[chip], AR, owner).start()
            received(w1_in, LS)

        @when(both(last_g, up_collector))
        def _():
            ar_in[chips - 1] = f_out[...]
            received(ar_in.at[pl.ds(0, chips - 1)], AR)
            x = tree([ar_in[i] for i in range(chips)])[:, :piece]
            w1_in[...] = fin[...] / (x * (states / total(jnp.sum(x, axis=0))))
            for i in range(chips - 1):
                copy(w1_in, w1_in, LS, start + CORES * i + 1).start()

        @when(no(up_collector))
        def _():
            received(col_in, CB)

        received(beta_in, BX)
        scaling = target / (alpha[...] * beta_in[...])

        @when(no(last_g))
        def _():
            received(w1_in, W1)

        b = backward(w1_in)
        set_beta(beta_last, b, w1_in[...])
        wait_down()

        @when(no(first_g))
        def _():
            w1_out[0] = scaling * beta_last[...]
            for i in low:
                to_group(w1_out.at[0], w1_in, W1, g - 1, i)

        copy(beta_last, beta_last, BO, mate).start()
        received(alpha_last, AO)

    @when(no(lead))
    def _():
        def send_b(b):
            b0_out[0:piece, :] = b
            b0_out[piece : piece + 1, :] = jnp.sum(b, axis=0, keepdims=True)
            wait_down()
            for i in low:
                to_group(b0_out, b0_in, B0, g - 1, i)

        @when(last_g)
        def _():
            send_b(rsum[...])
            received(col_in, CB)
            set_beta(beta, rsum[...], jnp.ones((chips, piece, LANES), jnp.float32))

        received(kernel.at[pl.ds(rows, rows)], KX)

        @when(no(last_g))
        def _():
            received(b0_in, B0)
            x = b0_in[...]
            s = total(tree([x[i, piece:] for i in range(chips)]))
            w0[...] = x[:, :piece] * (states / s)
            b = backward(w0)

            @when(no(first_g))
            def _():
                send_b(b)

            received(col_in, CB)
            set_beta(beta, b, w0[...])

        copy(beta, beta_in, BX, mate).start()
        alpha_last[...] = jnp.ones_like(alpha_last)
        alpha_in_value = jnp.ones((piece, LANES), jnp.float32)

        @when(first_g)
        def _():
            alpha_in[...] = alpha_in_value

        @when(no(first_g))
        def _():
            received(alpha_in, AX)
            received(f1_in, F1)
            a, s = sum_pieces(f1_in)
            alpha_last[...] = a * (states / s)

        copy(alpha_last, alpha_last, AO, mate).start()
        wait_up()

        @when(no(last_g))
        def _():
            scaling = target / (alpha_in[...] * beta[...])
            forward(scaling * alpha_last[...], high, lambda i: to_group(f_out.at[i], f1_in, F1, g + 1, i))

        received(beta_last, BO)

    result = target / (alpha_last[...] * beta_last[...])
    out[...] = jnp.where(lead, result[piece // CORES :], result[: piece // CORES])

    sent(row_in, RX)
    sent(marg.at[core], MX)
    sent(half, KX)

    @when(lead)
    def _():
        sent(beta_last, BO)

        @when(no(up_collector))
        def _():
            sent(col_out, CS)

        @when(up_collector)
        def _():
            sent(many, CB)

            @when(first_g)
            def _():
                sent(col_in, A1)

        @when(both(g > 0, no(last_g)))
        def _():
            sent(f0_in, F0)

        @when(no(first_g))
        def _():
            sent(alpha, AX)
            sent(w1_in, W1)

        @when(both(last_g, no(up_collector)))
        def _():
            sent(f_out, AR)

        @when(both(last_g, up_collector))
        def _():
            sent(many.at[pl.ds(0, chips - 1)], LS)

    @when(no(lead))
    def _():
        sent(col_out, PK)
        sent(beta, BX)
        sent(alpha_last, AO)

        @when(no(first_g))
        def _():
            sent(b0_in, B0)

        @when(no(last_g))
        def _():
            sent(f1_in, F1)


def solution(mesh):
    chain = mesh.shape["chain"]

    def on_device(cost, marginals, final_marginal):
        rows, states = cost.shape
        width = states // rows
        chips = width // CORES
        own = rows // LANES
        piece = CORES * own

        def buffer(*shape):
            return pltpu.VMEM(shape + (LANES,), jnp.float32)

        one = buffer(piece)
        whole = buffer(chips, piece)
        pieces = buffer(chips, piece + 1)
        scratch = dict(
            kernel=pltpu.VMEM((CORES * rows, states), jnp.float32), column=buffer(CORES * rows),
            marg=buffer(CORES, own), fin=whole, row_out=buffer(own), row_in=buffer(own), rsum=one,
            col_out=whole, col_mate=whole, col_in=whole, cs_in=buffer(chips, chips, piece),
            many=buffer(width - 1, chips, piece),
            a1_in=one, f_out=pieces, f0_in=pieces, f1_in=pieces, ar_in=buffer(chips, chips, piece + 1),
            b0_out=buffer(piece + 1), b0_in=pieces, w0=whole, w1_out=whole, w1_in=whole,
            alpha=one, alpha_in=one, beta=one, beta_in=one, alpha_last=one, beta_last=one,
            load_sem=pltpu.SemaphoreType.DMA((CHUNKS + 2,)), send_sem=pltpu.SemaphoreType.DMA((len(SLOTS),)),
            recv_sem=pltpu.SemaphoreType.DMA((len(SLOTS),)), token=pltpu.SemaphoreType.REGULAR((2,)),
        )
        scaling = pl.pallas_call(
            functools.partial(chain_kernel, width, chain // width),
            out_shape=jax.ShapeDtypeStruct((own, LANES), jnp.float32),
            in_specs=[pl.BlockSpec(memory_space=pl.ANY)] * 3,
            out_specs=pl.BlockSpec(memory_space=pltpu.VMEM),
            scratch_shapes=scratch,
            compiler_params=pltpu.CompilerParams(collective_id=0, has_side_effects=True),
            name="sinkhorn_chain",
        )(cost, marginals.reshape(own, LANES), final_marginal.reshape(chips, piece, LANES))
        return jnp.log(scaling).reshape(rows)

    placed = (P(("pop", "chain"), None), P(("pop", "chain")), P("pop"))
    return jax.shard_map(on_device, mesh=mesh, in_specs=placed, out_specs=P(("pop", "chain")), check_vma=False)
```

time: 415 us -> 92.8 us (0.22)
  the two profiles are of different devices: /device:TPU:44 before, /device:TPU:37 now
where the time goes in v2:
time: 92.8 us; the launch traced here: 92.7 us
  Pallas kernels  91.5 us (99%)
  local copies, waits for them, and re-layouts  1.25 us (1%)
    pallas_call x1, Pallas kernels, on_device(): pl.pallas_call(functools.partial(chain_kernel, width, chain // width), ou...  91.5 us

profile of v2, /device:TPU:37, one launch (start us, length us, event | category | flops | bytes accessed | tf_op | source)
XLA Modules:
  0.0 92.7 jit_solution(10520130724986249019)
XLA Ops:
  0.0 91.5 %sinkhorn_chain.1 = f32[2,128]{1,0:T(2,128)} custom-call(f32[256,4096]{1,0:T(8,128)} %cost.1, f32[2,128]{1,0:T(2,128)} %bitcast.5, f32[8,4,128]{2,1,0:T(4,128)} %bitcast.4), custom_call_target="tpu_custom_call" | custom-call | tf_op jit(solution)/shard_map/sinkhorn_chain/pallas_call | solution.py:496
  91.5 1.2 %log_bitcast_fusion = f32[256]{0:T(256)} fusion(f32[2,128]{1,0:T(2,128)} %sinkhorn_chain.1), kind=kLoop, calls=%fused_computation | loop fusion | bytes 2048 | tf_op jit(solution)/shard_map/reshape | solution.py:505

commit v3 on v2

--- a/solution.py
+++ b/solution.py
@@ -129,7 +129,7 @@
     def row_of_column(ref, count):
         parts = []
         for h in range(count):
-            x = ref[h * LANES : (h + 1) * LANES, :]
+            x = jnp.sum(ref[h * LANES : (h + 1) * LANES, :], axis=1, keepdims=True)
             parts.append(jnp.sum(jnp.where(eye(), x, 0.0), axis=0, keepdims=True))
         return jnp.concatenate(parts, axis=0)
 
@@ -168,11 +168,13 @@
 
         def step(r, carry):
             at = pl.ds(pl.multiple_of(r * SUBLANES, SUBLANES), SUBLANES)
-            x = tree([tree([kernel[at, lanes(b)] * ws[b] for b in range(q, q + 8)]) for q in range(0, blocks, 8)])
-            column[at, :] = jnp.broadcast_to(jnp.sum(x, axis=1, keepdims=True), (SUBLANES, LANES))
+            x = [kernel[at, lanes(b)] * ws[b] for b in range(4)]
+            for b in range(4, blocks):
+                x[b % 4] = x[b % 4] + kernel[at, lanes(b)] * ws[b]
+            column[at, :] = tree(x)
             return carry
 
-        lax.fori_loop(0, CORES * rows // SUBLANES, step, 0, unroll=4)
+        lax.fori_loop(0, CORES * rows // SUBLANES, step, 0, unroll=8)
         return row_of_column(column, piece)
 
     def sum_pieces(ref):
@@ -190,7 +192,7 @@
             xs.append(x)
             new.append(acc[b] + x)
         here = pl.ds(pl.multiple_of(r * SUBLANES, SUBLANES), SUBLANES)
-        column[here, :] = jnp.broadcast_to(jnp.sum(tree(xs), axis=1, keepdims=True), (SUBLANES, LANES))
+        column[here, :] = tree(xs)
         return tuple(new)
 
     acc = tuple(jnp.zeros((SUBLANES, LANES), jnp.float32) for _ in range(blocks))

time: 92.8 us -> 86.3 us (0.930)
  Pallas kernels: 91.5 us -> 84.9 us
    pallas_call x1, Pallas kernels: 91.5 us -> 84.9 us  [on_device(): pl.pallas_call(functools.partial(chain_kernel, width, chain // width), ou...]
where the time goes in v3:
time: 86.3 us; the launch traced here: 86.2 us
  Pallas kernels  84.9 us (98%)
  local copies, waits for them, and re-layouts  1.25 us (1%)
    pallas_call x1, Pallas kernels, on_device(): pl.pallas_call(functools.partial(chain_kernel, width, chain // width), ou...  84.9 us

profile of v3, /device:TPU:37, one launch (start us, length us, event | category | flops | bytes accessed | tf_op | source)
XLA Modules:
  0.0 86.2 jit_solution(6600247161748037311)
XLA Ops:
  0.0 84.9 %sinkhorn_chain.1 = f32[2,128]{1,0:T(2,128)} custom-call(f32[256,4096]{1,0:T(8,128)} %cost.1, f32[2,128]{1,0:T(2,128)} %bitcast.5, f32[8,4,128]{2,1,0:T(4,128)} %bitcast.4), custom_call_target="tpu_custom_call" | custom-call | tf_op jit(solution)/shard_map/sinkhorn_chain/pallas_call | solution.py:498
  84.9 1.2 %log_bitcast_fusion = f32[256]{0:T(256)} fusion(f32[2,128]{1,0:T(2,128)} %sinkhorn_chain.1), kind=kLoop, calls=%fused_computation | loop fusion | bytes 2048 | tf_op jit(solution)/shard_map/reshape | solution.py:507

commit v4 on v3

--- a/solution.py
+++ b/solution.py
@@ -15,8 +15,8 @@
 CORES = 2
 QUARTERS = 4
 MESH = pl.DeviceIdType.MESH
-SLOTS = range(17)
-KX, PK, RX, MX, CS, CB, A1, F0, AR, LS, B0, W1, F1, AX, BX, AO, BO = SLOTS
+SLOTS = range(16)
+KX, RX, MX, CS, CB, A1, F0, AR, LS, B0, W1, F1, AX, BX, AO, BO = SLOTS
 
 
 def eye():
@@ -40,7 +40,7 @@
 
 def chain_kernel(
     width, kernels, cost, marginals, final, out,
-    kernel, column, marg, fin, row_out, row_in, rsum, col_out, col_mate, col_in, cs_in, many,
+    kernel, column, marg, fin, row_out, row_in, rsum, col_out, col_in, cs_in, many,
     a1_in, f_out, f0_in, f1_in, ar_in, b0_out, b0_in, w0, w1_out, w1_in,
     alpha, alpha_in, beta, beta_in, alpha_last, beta_last,
     load_sem, send_sem, recv_sem, token,
@@ -49,6 +49,7 @@
     rows = kernel.shape[0] // CORES
     blocks = states // LANES
     piece = kernel.shape[0] // LANES
+    own = piece // CORES
     chips = width // CORES
     me = lax.axis_index("chain")
     g = me // width
@@ -105,8 +106,9 @@
 
     @when(up_collector)
     def _():
-        for i in range(1, chips - 1):
-            signal(barrier, start + CORES * i + 1)
+        for i in range(width - CORES):
+            if i != 1:
+                signal(barrier, start + i)
 
     span = rows // CHUNKS
     base = core * rows
@@ -126,9 +128,9 @@
     def lanes(b):
         return slice(b * LANES, (b + 1) * LANES)
 
-    def row_of_column(ref, count):
+    def row_of_column(ref, first, count):
         parts = []
-        for h in range(count):
+        for h in range(first, first + count):
             x = jnp.sum(ref[h * LANES : (h + 1) * LANES, :], axis=1, keepdims=True)
             parts.append(jnp.sum(jnp.where(eye(), x, 0.0), axis=0, keepdims=True))
         return jnp.concatenate(parts, axis=0)
@@ -161,10 +163,8 @@
             for i in targets:
                 send(i)
 
-    def backward(ref):
-        ws = [
-            jnp.broadcast_to(ref[b // piece, b % piece : b % piece + 1, :], (SUBLANES, LANES)) for b in range(blocks)
-        ]
+    def backward(w, emit):
+        ws = [jnp.broadcast_to(w(b), (SUBLANES, LANES)) for b in range(blocks)]
 
         def step(r, carry):
             at = pl.ds(pl.multiple_of(r * SUBLANES, SUBLANES), SUBLANES)
@@ -174,8 +174,9 @@
             column[at, :] = tree(x)
             return carry
 
-        lax.fori_loop(0, CORES * rows // SUBLANES, step, 0, unroll=8)
-        return row_of_column(column, piece)
+        for h in range(CORES):
+            lax.fori_loop(h * rows // SUBLANES, (h + 1) * rows // SUBLANES, step, 0, unroll=8)
+            emit(h, row_of_column(column, h * own, own))
 
     def sum_pieces(ref):
         x = tree([ref[i] for i in range(chips)])
@@ -201,37 +202,37 @@
         acc = lax.fori_loop(c * span // SUBLANES, (c + 1) * span // SUBLANES, chunk_step, acc)
     for b in range(blocks):
         col_out[b // piece, b % piece : b % piece + 1, :] = jnp.sum(acc[b], axis=0, keepdims=True)
-    row_out[...] = row_of_column(column, piece // CORES)
+    row_out[...] = row_of_column(column, 0, own)
     marg_load.wait()
     fin_load.wait()
 
-    greeted = jnp.where(lead, 2, 1)
+    greeted = jnp.where(mate == owner, 1, 2)
     greeted = jnp.where(down_collector, width - 1 + jnp.where(first_g, 0, width), greeted)
     greeted = jnp.where(up_collector, width - 1 + jnp.where(last_g, 0, width), greeted)
     pl.semaphore_wait(barrier, greeted)
 
-    @when(no(lead))
-    def _():
-        copy(col_out, col_mate, PK, mate).start()
+    UP, DOWN = 0, 1
+
+    @when(both(up_collector, no(last_g)))
+    def _():
+        for i in range(width - 1):
+            signal(token.at[UP], start + i)
+
+    @when(both(down_collector, no(first_g)))
+    def _():
+        for i in range(width):
+            if i != 1:
+                signal(token.at[DOWN], start + i)
+
+    @when(no(up_collector))
+    def _():
+        copy(col_out, cs_in.at[m], CS, owner).start()
 
     copy(row_out, row_in, RX, mate).start()
     copy(marg.at[core], marg.at[core], MX, mate).start()
     half = kernel.at[pl.ds(base, rows)]
     copy(half, half, KX, mate).start()
 
-    UP, DOWN = 0, 1
-
-    @when(both(up_collector, no(last_g)))
-    def _():
-        for i in range(width - 1):
-            signal(token.at[UP], start + i)
-
-    @when(both(down_collector, no(first_g)))
-    def _():
-        for i in range(width):
-            if i != 1:
-                signal(token.at[DOWN], start + i)
-
     def wait_up():
         @when(both(no(up_collector), no(last_g)))
         def _():
@@ -248,27 +249,18 @@
     high = list(range(chips - 1, -1, -1))
     low = list(range(chips))
 
-    @when(lead)
-    def _():
-        received(col_mate, PK)
-        col_out[...] = col_out[...] + col_mate[...]
-
-    @when(both(lead, no(up_collector)))
-    def _():
-        copy(col_out, cs_in.at[chip], CS, owner).start()
-
     @when(up_collector)
     def _():
-        cs_in[chips - 1] = col_out[...]
-        received(cs_in.at[pl.ds(0, chips - 1)], CS)
-        c = tree([cs_in[i] for i in range(chips)])
+        cs_in[width - 1] = col_out[...]
+        received(cs_in.at[pl.ds(0, width - 1)], CS)
+        c = tree([cs_in[i] for i in range(width)])
         col_in[...] = c
 
         @when(first_g)
         def _():
-            w1_out[...] = c * (states / total(jnp.sum(c, axis=0)))
+            w0[...] = c * (states / total(jnp.sum(c, axis=0)))
             for i in high:
-                copy(w1_out.at[i], a1_in, A1, start + width + CORES * i + 1).start()
+                copy(w0.at[i], a1_in, A1, start + width + CORES * i + 1).start()
 
         for i in range(width - 1):
             copy(col_in, col_in, CB, start + i).start()
@@ -286,9 +278,8 @@
     received(marg.at[1 - core], MX)
     target = jnp.concatenate([marg[i] for i in range(CORES)], axis=0)
 
-    def set_beta(ref, b, w):
-        s = total(jnp.sum(col_in[...] * w, axis=0))
-        ref[...] = b * (states / s)
+    def factor(products):
+        return states / total(jnp.sum(products, axis=0))
 
     @when(lead)
     def _():
@@ -315,12 +306,15 @@
                 def _():
                     to_group(f_out.at[i], f0_in, F0, g + 1, i)
 
+                @when(both(last_g, no(up_collector)))
+                def _():
+                    copy(f_out.at[i], ar_in.at[chip, i], AR, owner).start()
+
             forward(alpha[...], high, send)
             copy(alpha, alpha_in, AX, mate).start()
 
         @when(both(last_g, no(up_collector)))
         def _():
-            copy(f_out, ar_in.at[chip], AR, owner).start()
             received(w1_in, LS)
 
         @when(both(last_g, up_collector))
@@ -328,7 +322,9 @@
             ar_in[chips - 1] = f_out[...]
             received(ar_in.at[pl.ds(0, chips - 1)], AR)
             x = tree([ar_in[i] for i in range(chips)])[:, :piece]
-            w1_in[...] = fin[...] / (x * (states / total(jnp.sum(x, axis=0))))
+            x = fin[...] / (x * (states / total(jnp.sum(x, axis=0))))
+            for h in range(CORES):
+                w1_in[h] = x[:, h * own : (h + 1) * own]
             for i in range(chips - 1):
                 copy(w1_in, w1_in, LS, start + CORES * i + 1).start()
 
@@ -343,16 +339,20 @@
         def _():
             received(w1_in, W1)
 
-        b = backward(w1_in)
-        set_beta(beta_last, b, w1_in[...])
         wait_down()
 
-        @when(no(first_g))
-        def _():
-            w1_out[0] = scaling * beta_last[...]
-            for i in low:
-                to_group(w1_out.at[0], w1_in, W1, g - 1, i)
-
+        def send_w(h, b):
+            f = factor(sum(col_in[:, k * own : (k + 1) * own, :] * w1_in[k] for k in range(CORES)))
+            b = b * f
+            beta_last[h * own : (h + 1) * own, :] = b
+
+            @when(no(first_g))
+            def _():
+                w1_out[h, 0] = scaling[h * own : (h + 1) * own] * b
+                for i in low:
+                    copy(w1_out.at[h, 0], w1_in.at[h, chip], W1, start - width + CORES * i + core).start()
+
+        backward(lambda b: w1_in[b % piece // own, b // piece, b % own : b % own + 1, :], send_w)
         copy(beta_last, beta_last, BO, mate).start()
         received(alpha_last, AO)
 
@@ -369,7 +369,7 @@
         def _():
             send_b(rsum[...])
             received(col_in, CB)
-            set_beta(beta, rsum[...], jnp.ones((chips, piece, LANES), jnp.float32))
+            beta[...] = rsum[...] * factor(col_in[...])
 
         received(kernel.at[pl.ds(rows, rows)], KX)
 
@@ -379,14 +379,18 @@
             x = b0_in[...]
             s = total(tree([x[i, piece:] for i in range(chips)]))
             w0[...] = x[:, :piece] * (states / s)
-            b = backward(w0)
+
+            def keep(h, b):
+                beta[h * own : (h + 1) * own, :] = b
+
+            backward(lambda b: w0[b // piece, b % piece : b % piece + 1, :], keep)
 
             @when(no(first_g))
             def _():
-                send_b(b)
+                send_b(beta[...])
 
             received(col_in, CB)
-            set_beta(beta, b, w0[...])
+            beta[...] = beta[...] * factor(col_in[...] * w0[...])
 
         copy(beta, beta_in, BX, mate).start()
         alpha_last[...] = jnp.ones_like(alpha_last)
@@ -414,19 +418,19 @@
         received(beta_last, BO)
 
     result = target / (alpha_last[...] * beta_last[...])
-    out[...] = jnp.where(lead, result[piece // CORES :], result[: piece // CORES])
+    out[...] = jnp.where(lead, result[own:], result[:own])
 
     sent(row_in, RX)
     sent(marg.at[core], MX)
     sent(half, KX)
 
+    @when(no(up_collector))
+    def _():
+        sent(col_out, CS)
+
     @when(lead)
     def _():
         sent(beta_last, BO)
-
-        @when(no(up_collector))
-        def _():
-            sent(col_out, CS)
 
         @when(up_collector)
         def _():
@@ -455,7 +459,6 @@
 
     @when(no(lead))
     def _():
-        sent(col_out, PK)
         sent(beta, BX)
         sent(alpha_last, AO)
 
@@ -487,10 +490,10 @@
         scratch = dict(
             kernel=pltpu.VMEM((CORES * rows, states), jnp.float32), column=buffer(CORES * rows),
             marg=buffer(CORES, own), fin=whole, row_out=buffer(own), row_in=buffer(own), rsum=one,
-            col_out=whole, col_mate=whole, col_in=whole, cs_in=buffer(chips, chips, piece),
+            col_out=whole, col_in=whole, cs_in=buffer(width, chips, piece),
             many=buffer(width - 1, chips, piece),
             a1_in=one, f_out=pieces, f0_in=pieces, f1_in=pieces, ar_in=buffer(chips, chips, piece + 1),
-            b0_out=buffer(piece + 1), b0_in=pieces, w0=whole, w1_out=whole, w1_in=whole,
+            b0_out=buffer(piece + 1), b0_in=pieces, w0=whole, w1_out=buffer(CORES, chips, own), w1_in=buffer(CORES, chips, own),
             alpha=one, alpha_in=one, beta=one, beta_in=one, alpha_last=one, beta_last=one,
             load_sem=pltpu.SemaphoreType.DMA((CHUNKS + 2,)), send_sem=pltpu.SemaphoreType.DMA((len(SLOTS),)),
             recv_sem=pltpu.SemaphoreType.DMA((len(SLOTS),)), token=pltpu.SemaphoreType.REGULAR((2,)),

time: 86.3 us -> 85.5 us (level)
  no operation moved by 1% of the time
where the time goes in v4:
time: 85.5 us; the launch traced here: 85.4 us
  Pallas kernels  84.1 us (98%)
  local copies, waits for them, and re-layouts  1.25 us (1%)
    pallas_call x1, Pallas kernels, on_device(): pl.pallas_call(functools.partial(chain_kernel, width, chain // width), ou...  84.1 us

profile of v4, /device:TPU:37, one launch (start us, length us, event | category | flops | bytes accessed | tf_op | source)
XLA Modules:
  0.0 85.4 jit_solution(11124317387412767756)
XLA Ops:
  0.0 84.1 %sinkhorn_chain.1 = f32[2,128]{1,0:T(2,128)} custom-call(f32[256,4096]{1,0:T(8,128)} %cost.1, f32[2,128]{1,0:T(2,128)} %bitcast.5, f32[8,4,128]{2,1,0:T(4,128)} %bitcast.4), custom_call_target="tpu_custom_call" | custom-call | tf_op jit(solution)/shard_map/sinkhorn_chain/pallas_call | solution.py:501
  84.1 1.2 %log_bitcast_fusion = f32[256]{0:T(256)} fusion(f32[2,128]{1,0:T(2,128)} %sinkhorn_chain.1), kind=kLoop, calls=%fused_computation | loop fusion | bytes 2048 | tf_op jit(solution)/shard_map/reshape | solution.py:510

commit v5 on v4

--- a/solution.py
+++ b/solution.py
@@ -85,31 +85,6 @@
     def sent(ref, slot):
         copy(ref, ref, slot, mate).wait_send()
 
-    barrier = pltpu.get_barrier_semaphore()
-    signal(barrier, mate)
-
-    @when(both(me != owner, mate != owner))
-    def _():
-        signal(barrier, owner)
-
-    @when(both(me != start + 1, mate != start + 1))
-    def _():
-        signal(barrier, start + 1)
-
-    @when(no(first_g))
-    def _():
-        signal(barrier, owner - width)
-
-    @when(no(last_g))
-    def _():
-        signal(barrier, start + width + 1)
-
-    @when(up_collector)
-    def _():
-        for i in range(width - CORES):
-            if i != 1:
-                signal(barrier, start + i)
-
     span = rows // CHUNKS
     base = core * rows
 
@@ -124,6 +99,31 @@
     fin_load = pltpu.make_async_copy(final, fin, load_sem.at[CHUNKS + 1])
     marg_load.start()
     fin_load.start()
+
+    barrier = pltpu.get_barrier_semaphore()
+    signal(barrier, mate)
+
+    @when(both(me != owner, mate != owner))
+    def _():
+        signal(barrier, owner)
+
+    @when(both(me != start + 1, mate != start + 1))
+    def _():
+        signal(barrier, start + 1)
+
+    @when(no(first_g))
+    def _():
+        signal(barrier, owner - width)
+
+    @when(no(last_g))
+    def _():
+        signal(barrier, start + width + 1)
+
+    @when(up_collector)
+    def _():
+        for i in range(width - CORES):
+            if i != 1:
+                signal(barrier, start + i)
 
     def lanes(b):
         return slice(b * LANES, (b + 1) * LANES)
@@ -202,9 +202,6 @@
         acc = lax.fori_loop(c * span // SUBLANES, (c + 1) * span // SUBLANES, chunk_step, acc)
     for b in range(blocks):
         col_out[b // piece, b % piece : b % piece + 1, :] = jnp.sum(acc[b], axis=0, keepdims=True)
-    row_out[...] = row_of_column(column, 0, own)
-    marg_load.wait()
-    fin_load.wait()
 
     greeted = jnp.where(mate == owner, 1, 2)
     greeted = jnp.where(down_collector, width - 1 + jnp.where(first_g, 0, width), greeted)
@@ -228,6 +225,9 @@
     def _():
         copy(col_out, cs_in.at[m], CS, owner).start()
 
+    row_out[...] = row_of_column(column, 0, own)
+    marg_load.wait()
+    fin_load.wait()
     copy(row_out, row_in, RX, mate).start()
     copy(marg.at[core], marg.at[core], MX, mate).start()
     half = kernel.at[pl.ds(base, rows)]
@@ -308,7 +308,7 @@
 
                 @when(both(last_g, no(up_collector)))
                 def _():
-                    copy(f_out.at[i], ar_in.at[chip, i], AR, owner).start()
+                    copy(f_out.at[i, pl.ds(0, piece)], ar_in.at[chip, i], AR, owner).start()
 
             forward(alpha[...], high, send)
             copy(alpha, alpha_in, AX, mate).start()
@@ -319,9 +319,9 @@
 
         @when(both(last_g, up_collector))
         def _():
-            ar_in[chips - 1] = f_out[...]
+            ar_in[chips - 1] = f_out[:, :piece, :]
             received(ar_in.at[pl.ds(0, chips - 1)], AR)
-            x = tree([ar_in[i] for i in range(chips)])[:, :piece]
+            x = tree([ar_in[i] for i in range(chips)])
             x = fin[...] / (x * (states / total(jnp.sum(x, axis=0))))
             for h in range(CORES):
                 w1_in[h] = x[:, h * own : (h + 1) * own]
@@ -344,7 +344,9 @@
         def send_w(h, b):
             f = factor(sum(col_in[:, k * own : (k + 1) * own, :] * w1_in[k] for k in range(CORES)))
             b = b * f
-            beta_last[h * own : (h + 1) * own, :] = b
+            beta_last[h] = b
+            if h == 0:
+                copy(beta_last.at[0], beta_last.at[0], BO, mate).start()
 
             @when(no(first_g))
             def _():
@@ -353,8 +355,8 @@
                     copy(w1_out.at[h, 0], w1_in.at[h, chip], W1, start - width + CORES * i + core).start()
 
         backward(lambda b: w1_in[b % piece // own, b // piece, b % own : b % own + 1, :], send_w)
-        copy(beta_last, beta_last, BO, mate).start()
         received(alpha_last, AO)
+        out[...] = target[own:] / (alpha_last[own:, :] * beta_last[1])
 
     @when(no(lead))
     def _():
@@ -415,10 +417,8 @@
             scaling = target / (alpha_in[...] * beta[...])
             forward(scaling * alpha_last[...], high, lambda i: to_group(f_out.at[i], f1_in, F1, g + 1, i))
 
-        received(beta_last, BO)
-
-    result = target / (alpha_last[...] * beta_last[...])
-    out[...] = jnp.where(lead, result[own:], result[:own])
+        received(beta_last.at[0], BO)
+        out[...] = target[:own] / (alpha_last[:own, :] * beta_last[0])
 
     sent(row_in, RX)
     sent(marg.at[core], MX)
@@ -430,7 +430,7 @@
 
     @when(lead)
     def _():
-        sent(beta_last, BO)
+        sent(beta_last.at[0], BO)
 
         @when(up_collector)
         def _():
@@ -451,7 +451,7 @@
 
         @when(both(last_g, no(up_collector)))
         def _():
-            sent(f_out, AR)
+            sent(w0, AR)
 
         @when(both(last_g, up_collector))
         def _():
@@ -492,9 +492,9 @@
             marg=buffer(CORES, own), fin=whole, row_out=buffer(own), row_in=buffer(own), rsum=one,
             col_out=whole, col_in=whole, cs_in=buffer(width, chips, piece),
             many=buffer(width - 1, chips, piece),
-            a1_in=one, f_out=pieces, f0_in=pieces, f1_in=pieces, ar_in=buffer(chips, chips, piece + 1),
+            a1_in=one, f_out=pieces, f0_in=pieces, f1_in=pieces, ar_in=buffer(chips, chips, piece),
             b0_out=buffer(piece + 1), b0_in=pieces, w0=whole, w1_out=buffer(CORES, chips, own), w1_in=buffer(CORES, chips, own),
-            alpha=one, alpha_in=one, beta=one, beta_in=one, alpha_last=one, beta_last=one,
+            alpha=one, alpha_in=one, beta=one, beta_in=one, alpha_last=one, beta_last=buffer(CORES, own),
             load_sem=pltpu.SemaphoreType.DMA((CHUNKS + 2,)), send_sem=pltpu.SemaphoreType.DMA((len(SLOTS),)),
             recv_sem=pltpu.SemaphoreType.DMA((len(SLOTS),)), token=pltpu.SemaphoreType.REGULAR((2,)),
         )

time: 85.5 us -> 85 us (level)
  no operation moved by 1% of the time
where the time goes in v5:
time: 85 us; the launch traced here: 84.8 us
  Pallas kernels  83.6 us (98%)
  local copies, waits for them, and re-layouts  1.25 us (1%)
    pallas_call x1, Pallas kernels, on_device(): pl.pallas_call(functools.partial(chain_kernel, width, chain // width), ou...  83.6 us

profile of v5, /device:TPU:37, one launch (start us, length us, event | category | flops | bytes accessed | tf_op | source)
XLA Modules:
  0.0 84.8 jit_solution(15169866371288421018)
XLA Ops:
  0.0 83.6 %sinkhorn_chain.1 = f32[2,128]{1,0:T(2,128)} custom-call(f32[256,4096]{1,0:T(8,128)} %cost.1, f32[2,128]{1,0:T(2,128)} %bitcast.5, f32[8,4,128]{2,1,0:T(4,128)} %bitcast.4), custom_call_target="tpu_custom_call" | custom-call | tf_op jit(solution)/shard_map/sinkhorn_chain/pallas_call | solution.py:501
  83.6 1.2 %log_bitcast_fusion = f32[256]{0:T(256)} fusion(f32[2,128]{1,0:T(2,128)} %sinkhorn_chain.1), kind=kLoop, calls=%fused_computation | loop fusion | bytes 2048 | tf_op jit(solution)/shard_map/reshape | solution.py:510

commit v6 on v5

--- a/solution.py
+++ b/solution.py
@@ -11,7 +11,7 @@
 ENTROPIC = 0.25
 LANES = 128
 SUBLANES = 8
-CHUNKS = 8
+CHUNKS = 16
 CORES = 2
 QUARTERS = 4
 MESH = pl.DeviceIdType.MESH
@@ -155,7 +155,7 @@
                 return tuple(a + kernel[at, lanes(b)] * v for a, b in zip(acc, mine))
 
             zero = tuple(jnp.zeros((SUBLANES, LANES), jnp.float32) for _ in mine)
-            acc = lax.fori_loop(0, CORES * rows // SUBLANES, step, zero, unroll=8)
+            acc = lax.fori_loop(0, CORES * rows // SUBLANES, step, zero, unroll=16)
             for n, i in enumerate(targets):
                 for h in range(piece):
                     f_out[i, h : h + 1, :] = jnp.sum(acc[n * piece + h], axis=0, keepdims=True)
@@ -500,7 +500,7 @@
         )
         scaling = pl.pallas_call(
             functools.partial(chain_kernel, width, chain // width),
-            out_shape=jax.ShapeDtypeStruct((own, LANES), jnp.float32),
+            out_shape=pltpu.VMEM((own, LANES), jnp.float32),
             in_specs=[pl.BlockSpec(memory_space=pl.ANY)] * 3,
             out_specs=pl.BlockSpec(memory_space=pltpu.VMEM),
             scratch_shapes=scratch,

time: 85 us -> 83.7 us (0.985)
  no operation moved by 1% of the time
where the time goes in v6:
time: 83.7 us; the launch traced here: 83.5 us
  Pallas kernels  83 us (99%)
    pallas_call x1, Pallas kernels, on_device(): pl.pallas_call(functools.partial(chain_kernel, width, chain // width), ou...  83 us

profile of v6, /device:TPU:37, one launch (start us, length us, event | category | flops | bytes accessed | tf_op | source)
XLA Modules:
  0.0 83.5 jit_solution(11612897082064413910)
XLA Ops:
  0.0 83.0 %sinkhorn_chain.1 = f32[2,128]{1,0:T(2,128)S(1)} custom-call(f32[256,4096]{1,0:T(8,128)} %cost.1, f32[2,128]{1,0:T(2,128)} %bitcast.5, f32[8,4,128]{2,1,0:T(4,128)} %bitcast.4), custom_call_target="tpu_custom_call" | custom-call | tf_op jit(solution)/shard_map/sinkhorn_chain/pallas_call | solution.py:501
  83.0 0.6 log_bitcast_fusion

commit v7 on v6

--- a/solution.py
+++ b/solution.py
@@ -14,6 +14,7 @@
 CHUNKS = 16
 CORES = 2
 QUARTERS = 4
+OWNERS = 2
 MESH = pl.DeviceIdType.MESH
 SLOTS = range(16)
 KX, RX, MX, CS, CB, A1, F0, AR, LS, B0, W1, F1, AX, BX, AO, BO = SLOTS
@@ -63,6 +64,7 @@
     up_collector = jnp.logical_and(lead, chip == chips - 1)
     down_collector = jnp.logical_and(lead, chip == 0)
     owner = start + width - 1
+    share = chips // OWNERS
 
     def when(condition):
         return pl.when(condition)
@@ -298,6 +300,7 @@
 
         received(kernel.at[pl.ds(0, rows)], KX)
         wait_up()
+        wait_down()
 
         @when(no(first_g))
         def _():
@@ -306,27 +309,36 @@
                 def _():
                     to_group(f_out.at[i], f0_in, F0, g + 1, i)
 
-                @when(both(last_g, no(up_collector)))
+                taker = chips - OWNERS + i // share
+
+                @when(both(last_g, chip != taker))
                 def _():
-                    copy(f_out.at[i, pl.ds(0, piece)], ar_in.at[chip, i], AR, owner).start()
+                    copy(f_out.at[i], ar_in.at[chip, i % share], AR, start + CORES * taker + 1).start()
 
             forward(alpha[...], high, send)
             copy(alpha, alpha_in, AX, mate).start()
 
-        @when(both(last_g, no(up_collector)))
+        for o in range(OWNERS):
+            taker = chips - OWNERS + o
+            part = pl.ds(o * share, share)
+
+            @when(both(last_g, chip == taker))
+            def _():
+                ar_in[taker] = f_out[part]
+                received(ar_in.at[pl.ds(0, chips - 1)], AR)
+                x = tree([ar_in[i] for i in range(chips)])
+                x = fin[part] / (x[:, :piece] * (states / total(x[0, piece:])))
+                for h in range(CORES):
+                    w1_in[h, part] = x[:, h * own : (h + 1) * own]
+                for i in range(chips):
+                    for h in range(CORES):
+                        if i != taker:
+                            copy(w1_in.at[h, part], w1_in.at[h, part], LS, start + CORES * i + 1).start()
+                received(w1_in.at[0], LS)
+
+        @when(both(last_g, chip < chips - OWNERS))
         def _():
             received(w1_in, LS)
-
-        @when(both(last_g, up_collector))
-        def _():
-            ar_in[chips - 1] = f_out[:, :piece, :]
-            received(ar_in.at[pl.ds(0, chips - 1)], AR)
-            x = tree([ar_in[i] for i in range(chips)])
-            x = fin[...] / (x * (states / total(jnp.sum(x, axis=0))))
-            for h in range(CORES):
-                w1_in[h] = x[:, h * own : (h + 1) * own]
-            for i in range(chips - 1):
-                copy(w1_in, w1_in, LS, start + CORES * i + 1).start()
 
         @when(no(up_collector))
         def _():
@@ -338,8 +350,6 @@
         @when(no(last_g))
         def _():
             received(w1_in, W1)
-
-        wait_down()
 
         def send_w(h, b):
             f = factor(sum(col_in[:, k * own : (k + 1) * own, :] * w1_in[k] for k in range(CORES)))
@@ -449,13 +459,14 @@
             sent(alpha, AX)
             sent(w1_in, W1)
 
-        @when(both(last_g, no(up_collector)))
-        def _():
-            sent(w0, AR)
-
-        @when(both(last_g, up_collector))
-        def _():
-            sent(many.at[pl.ds(0, chips - 1)], LS)
+        @when(both(last_g, chip < chips - OWNERS))
+        def _():
+            sent(f_out, AR)
+
+        @when(both(last_g, chip >= chips - OWNERS))
+        def _():
+            sent(f_out.at[pl.ds(0, share)], AR)
+            sent(many.at[pl.ds(0, chips - 1), pl.ds(0, share)], LS)
 
     @when(no(lead))
     def _():
@@ -492,7 +503,7 @@
             marg=buffer(CORES, own), fin=whole, row_out=buffer(own), row_in=buffer(own), rsum=one,
             col_out=whole, col_in=whole, cs_in=buffer(width, chips, piece),
             many=buffer(width - 1, chips, piece),
-            a1_in=one, f_out=pieces, f0_in=pieces, f1_in=pieces, ar_in=buffer(chips, chips, piece),
+            a1_in=one, f_out=pieces, f0_in=pieces, f1_in=pieces, ar_in=buffer(chips, chips // OWNERS, piece + 1),
             b0_out=buffer(piece + 1), b0_in=pieces, w0=whole, w1_out=buffer(CORES, chips, own), w1_in=buffer(CORES, chips, own),
             alpha=one, alpha_in=one, beta=one, beta_in=one, alpha_last=one, beta_last=buffer(CORES, own),
             load_sem=pltpu.SemaphoreType.DMA((CHUNKS + 2,)), send_sem=pltpu.SemaphoreType.DMA((len(SLOTS),)),

time: 83.7 us -> 82.7 us (0.988)
  Pallas kernels: 83 us -> 82.1 us
    pallas_call x1, Pallas kernels: 83 us -> 82.1 us  [on_device(): pl.pallas_call(functools.partial(chain_kernel, width, chain // width), ou...]
where the time goes in v7:
time: 82.7 us; the launch traced here: 82.6 us
  Pallas kernels  82.1 us (99%)
    pallas_call x1, Pallas kernels, on_device(): pl.pallas_call(functools.partial(chain_kernel, width, chain // width), ou...  82.1 us

profile of v7, /device:TPU:37, one launch (start us, length us, event | category | flops | bytes accessed | tf_op | source)
XLA Modules:
  0.0 82.6 jit_solution(11502414177920204784)
XLA Ops:
  0.0 82.1 %sinkhorn_chain.1 = f32[2,128]{1,0:T(2,128)S(1)} custom-call(f32[256,4096]{1,0:T(8,128)} %cost.1, f32[2,128]{1,0:T(2,128)} %bitcast.5, f32[8,4,128]{2,1,0:T(4,128)} %bitcast.4), custom_call_target="tpu_custom_call" | custom-call | tf_op jit(solution)/shard_map/sinkhorn_chain/pallas_call | solution.py:512
  82.1 0.6 log_bitcast_fusion
